TPU v7x, 32 devices: a whole 2x2x4 slice. The times are simulated.
32 devices in a mesh: band: 8 (over z, x), sub: 4 (over y, core).
Axes of the slice: x: 2, y: 2, z: 4, core: 2. Of those that a mesh axis runs over, the one named last changes fastest.
Arguments:
- grad_pred: bfloat16 [227, 24576], P(None, ('band', 'sub')), may hold values from -6 to 6
- grid_latent: bfloat16 [24576, 512], P(('band', 'sub')), may hold values from -6 to 6
- mesh_latent: bfloat16 [10240, 512], P(('band', 'sub')), may hold values from -6 to 6
- send_slot: int32 [24576], P(('band', 'sub')), may hold values from 0 to 2303, as said below
- edge_src: int32 [3, 73728], P(None, ('band', 'sub')), may hold values from 0 to 10239, as said below
- w_mesh: bfloat16 [512, 512], replicated, may hold values from -0.25 to 0.25
- w_grid: bfloat16 [512, 512], replicated, may hold values from -0.25 to 0.25
- w_msg: bfloat16 [512, 512], replicated, may hold values from -0.25 to 0.25
- w_out: bfloat16 [512, 227], replicated, may hold values from -0.25 to 0.25
Outputs:
- mesh_grad: bfloat16 [10240, 512], P(('band', 'sub'))
- grad_w_mesh: float32 [512, 512], replicated
- grad_w_grid: float32 [512, 512], replicated
- grad_w_msg: float32 [512, 512], replicated
- grad_w_out: float32 [512, 227], replicated
Inputs may be any that keep to these rules, and one draw needn't show every extreme that they name: For grid point p on latitude-major device i, send_slot[p] = j * 72 + r names patch-major device j and a rank r. On one device i the values are distinct, and for each j the ranks used are 0 to the count of i's points sent to j minus 1. Every such count is at most 72, and 72 is reached in every draw. Every grid point thereby gets one patch-major slot; live slots of each source stand at the front of its block of 72. One patch-major device holds at most 1920 live slots, reached on some device in every draw. `edge_src`: A slot on patch-major device j, of band b = j // 4, names senders in patch b only: mesh rows b * 1280 to (b + 1) * 1280 - 1. Entries of empty slots lie in that range too and are not read.
All inputs are finite; a program needn't handle non-finite values.
Results may differ from a plain program's by a relative error of at most 0.0076.
Values may be sent and summed in bfloat16 or wider, within the bound.
No kernel may reach another device: no remote copies, remote signals or barrier semaphores. Data moves between devices by JAX's collectives and lax.ppermute only.
A program may use at most 128 MiB of HBM per device.

v0:
```python
import math

import jax
import jax.numpy as jnp
from jax import lax
from jax.sharding import PartitionSpec as P


def latitude_weight(points, total):
    angle = jnp.pi * ((points.astype(jnp.float32) + 0.5) / total - 0.5)
    return 0.5 * jnp.pi * jnp.cos(angle)


def silu_slope(value):
    sigma = jax.nn.sigmoid(value)
    return sigma * (1.0 + value * (1.0 - sigma))


def contract_rows(left, right):
    return lax.dot_general(
        left, right, (((0,), (0,)), ((), ())), preferred_element_type=jnp.float32
    )


def times_transpose(left, right):
    return lax.dot_general(
        left, right, (((1,), (1,)), ((), ())), preferred_element_type=jnp.float32
    )


def shards(grad_pred, grid_latent, mesh_latent, send_slot, edge_src, w_mesh, w_grid, w_msg, w_out):
    grid_rows = grid_latent.shape[0]
    width = grid_latent.shape[1]
    channels = grad_pred.shape[0]
    devices = lax.axis_size(("band", "sub"))
    capacity = 3 * grid_rows // devices
    total_points = grid_rows * devices
    own_index = lax.axis_index(("band", "sub"))
    points = own_index * grid_rows + jnp.arange(grid_rows, dtype=jnp.int32)
    weighted = (
        latitude_weight(points, total_points)[None, :] * grad_pred.astype(jnp.float32)
    ).astype(jnp.bfloat16)
    target = send_slot // capacity
    slot_rank = send_slot % capacity
    joined = jnp.concatenate([grid_latent, weighted.T], axis=1)
    row_width = width + channels
    send_buffer = (
        jnp.zeros((devices, capacity, row_width), jnp.bfloat16).at[target, slot_rank].set(joined)
    )
    received = lax.all_to_all(send_buffer, ("band", "sub"), split_axis=0, concat_axis=0, tiled=True)
    slots = devices * capacity
    slot_rows = received.reshape(slots, row_width)
    latent_rows = slot_rows[:, :width]
    grad_rows = slot_rows[:, width:]
    grid_proj = jnp.dot(latent_rows, w_grid, preferred_element_type=jnp.float32).astype(
        jnp.bfloat16
    )
    mesh_proj = jnp.dot(mesh_latent, w_mesh, preferred_element_type=jnp.float32).astype(
        jnp.bfloat16
    )
    patch_proj = lax.all_gather(mesh_proj, "sub", axis=0, tiled=True)
    patch_size = patch_proj.shape[0]
    band_index = lax.axis_index("band")
    local_node = edge_src - band_index * patch_size
    grid_float = grid_proj.astype(jnp.float32)
    pre_acts = [
        patch_proj[local_node[corner]].astype(jnp.float32) + grid_float for corner in range(3)
    ]
    act_sum = (
        jax.nn.silu(pre_acts[0]) + jax.nn.silu(pre_acts[1]) + jax.nn.silu(pre_acts[2])
    ).astype(jnp.bfloat16)
    aggregate = jnp.dot(act_sum, w_msg, preferred_element_type=jnp.float32).astype(jnp.bfloat16)
    out_part = contract_rows(aggregate, grad_rows)
    agg_rows = times_transpose(grad_rows, w_out).astype(jnp.bfloat16)
    msg_part = contract_rows(act_sum, agg_rows)
    out_total = lax.psum(out_part, ("band", "sub"))
    msg_total = lax.psum(msg_part, ("band", "sub"))
    act_grad = times_transpose(agg_rows, w_msg)
    pre_grads = [(act_grad * silu_slope(pre)).astype(jnp.bfloat16) for pre in pre_acts]
    grid_proj_grad = (
        pre_grads[0].astype(jnp.float32)
        + pre_grads[1].astype(jnp.float32)
        + pre_grads[2].astype(jnp.float32)
    ).astype(jnp.bfloat16)
    node_part = jnp.zeros((patch_size, width), jnp.float32)
    for corner in range(3):
        node_part = node_part.at[local_node[corner]].add(pre_grads[corner].astype(jnp.float32))
    node_total = lax.psum_scatter(node_part, "sub", scatter_dimension=0, tiled=True)
    grid_part = contract_rows(latent_rows, grid_proj_grad)
    mesh_proj_grad = node_total.astype(jnp.bfloat16)
    mesh_grad = times_transpose(mesh_proj_grad, w_mesh).astype(jnp.bfloat16)
    mesh_part = contract_rows(mesh_latent, mesh_proj_grad)
    grad_scale = 1.0 / math.sqrt(3.0 * total_points)
    grid_total = lax.psum(grid_part, ("band", "sub"))
    mesh_total = lax.psum(mesh_part, ("band", "sub"))
    return (
        mesh_grad,
        mesh_total * grad_scale,
        grid_total * grad_scale,
        msg_total * grad_scale,
        out_total * grad_scale,
    )


def solution(mesh):
    placed = (
        P(None, ("band", "sub")),
        P(("band", "sub"), None),
        P(("band", "sub"), None),
        P(("band", "sub")),
        P(None, ("band", "sub")),
        P(),
        P(),
        P(),
        P(),
    )
    return jax.shard_map(
        shards,
        mesh=mesh,
        in_specs=placed,
        out_specs=(P(("band", "sub"), None), P(), P(), P(), P()),
        check_vma=False,
    )
```

profile of v0, /device:TPU:0, one launch (start us, length us, event | category | flops | bytes accessed | tf_op | source)
XLA Modules:
  0.0 467.2 jit_solution(4389432427457058807)
XLA Ops:
  7.2 0.8 compare_select_fusion.4
  8.0 1.0 fusion.15
  9.2 1.2 pad_maximum_fusion
  10.5 2.0 broadcast_in_dim.9
  12.5 101.5 %scatter_fusion = bf16[32,72,739]{2,1,0:T(8,128)(2,1)} fusion(bf16[32,72,739]{2,1,0:T(8,128)(2,1)} %broadcast_in_dim.9, s32[768]{0:T(1024)S(1)} %fusion.23, bf16[768,739]{1,0:T(8,128)(2,1)S(1)} %pad_maximum_fusion), kind=kCustom, calls=%fused_computation.3 | custom fusion | bytes 3411456 | tf_op jit(solution)/shard_map/scatter | solution.py:48
  114.1 7.4 %all-to-all-start = ((bf16[32,72,739]{2,1,0:T(8,128)(2,1)}), bf16[32,72,739]{2,1,0:T(8,128)(2,1)}, u32[]{:S(2)}, u32[]{:S(2)}) async-start(bf16[32,72,739]{2,1,0:T(8,128)(2,1)} %scatter_fusion), calls=%async_computation | async-start | bytes 7077888 | tf_op jit(solution)/shard_map/all_to_all | solution.py:50
  121.5 1.1 convolution_convert_fusion.4
  122.8 33.9 %all-gather.2.cloned.1.call-done = bf16[1280,512]{1,0:T(8,128)(2,1)} async-done(((bf16[320,512]{1,0:T(8,128)(2,1)}), bf16[1280,512]{1,0:T(8,128)(2,1)}) %all-gather.2.cloned.1.call-update) | async-done | bytes 1310736 | tf_op jit(solution)/shard_map/all_gather | solution.py:61
  156.8 9.2 %gather_fusion.2 = bf16[2304,512]{1,0:T(8,128)(2,1)} fusion(bf16[1280,512]{1,0:T(8,128)(2,1)} %all-gather.2.cloned.1.call-done, s32[3072]{0:T(1024)S(1)} %get-tuple-element.33), kind=kCustom, calls=%fused_computation.2 | custom fusion | bytes 4727808 | tf_op jit(solution)/shard_map/gather | solution.py:67
  166.0 7.5 %gather_fusion.1 = bf16[2304,512]{1,0:T(8,128)(2,1)} fusion(bf16[1280,512]{1,0:T(8,128)(2,1)S(1)} %copy-done.1, s32[3072]{0:T(1024)S(1)} %get-tuple-element.34), kind=kCustom, calls=%fused_computation.1 | custom fusion | bytes 4727808 | tf_op jit(solution)/shard_map/gather | solution.py:67
  173.5 7.5 %gather_fusion = bf16[2304,512]{1,0:T(8,128)(2,1)} fusion(bf16[1280,512]{1,0:T(8,128)(2,1)S(1)} %copy-done.1, s32[3072]{0:T(1024)S(1)} %pad_clamp_fusion.2), kind=kCustom, calls=%fused_computation | custom fusion | bytes 4727808 | tf_op jit(solution)/shard_map/gather | solution.py:67
  181.0 20.5 %all-to-all-done = bf16[32,72,739]{2,1,0:T(8,128)(2,1)} async-done(((bf16[32,72,739]{2,1,0:T(8,128)(2,1)}), bf16[32,72,739]{2,1,0:T(8,128)(2,1)}, u32[]{:S(2)}, u32[]{:S(2)}) %all-to-all-start) | async-done | bytes 3405344 | tf_op jit(solution)/shard_map/all_to_all | solution.py:50
  201.5 2.0 convolution_convert_fusion.2
  203.6 3.9 convolution_convert_fusion.1
  208.3 9.1 %multiply_convert_fusion = (bf16[2304,512]{1,0:T(8,128)(2,1)}, bf16[2304,512]{1,0:T(8,128)(2,1)}, bf16[2304,512]{1,0:T(8,128)(2,1)}, bf16[2304,512]{1,0:T(8,128)(2,1)}) fusion(bf16[2304,512]{1,0:T(8,128)(2,1)S(1)} %convolution_convert_fusion.1, bf16[2304,512]{1,0:T(8,128)(2,1)S(1)} %copy-done.6, bf16[2304,512]{1,0:T(8,128)(2,1)S(1)} %copy-done.7, ...), kind=kOutput, calls=%fused_computation.20 | convolution fusion | flops 1255145472 | bytes 21757952 | tf_op jit(solution)/shard_map/dot_general | solution.py:26
  217.3 17.0 %scatter_custom_fusion.1 = f32[1280,512]{1,0:T(8,128)S(1)} fusion(s32[2304]{0:T(1024)S(1)} %get-tuple-element.22, bf16[2304,512]{1,0:T(8,128)(2,1)} %get-tuple-element.30, f32[]{:T(128)} %constant.20.clone.1), kind=kCustom, calls=%fused_computation.16 | custom fusion | flops 2359296 | bytes 4980740 | tf_op jit(solution)/shard_map/scatter-add | solution.py:87
  234.3 17.5 %scatter_custom_fusion.2 = f32[1280,512]{1,0:T(8,128)S(1)} fusion(f32[1280,512]{1,0:T(8,128)S(1)} %scatter_custom_fusion.1, s32[2304]{0:T(1024)S(1)} %get-tuple-element.21, bf16[2304,512]{1,0:T(8,128)(2,1)} %get-tuple-element.28), kind=kCustom, calls=%fused_computation.14 | custom fusion | flops 2359296 | bytes 4980736 | tf_op jit(solution)/shard_map/scatter-add | solution.py:87
  251.9 17.4 %scatter_custom_fusion.3 = f32[1280,512]{1,0:T(8,128)S(1)} fusion(f32[1280,512]{1,0:T(8,128)S(1)} %scatter_custom_fusion.2, s32[2304]{0:T(1024)S(1)} %get-tuple-element.20, bf16[2304,512]{1,0:T(8,128)(2,1)} %get-tuple-element.27), kind=kCustom, calls=%fused_computation.11 | custom fusion | flops 2359296 | bytes 4980736 | tf_op jit(solution)/shard_map/scatter-add | solution.py:87
  269.3 1.5 copy-done.2
  271.0 4.8 %fusion.24 = f32[512,512]{0,1:T(8,128)} fusion(bf16[2304,512]{1,0:T(8,128)(2,1)} %get-tuple-element.29, bf16[2304,512]{1,0:T(8,128)(2,1)} %copy-done.5), kind=kOutput, calls=%fused_computation.74 | convolution fusion | flops 1207959552 | bytes 5767168 | tf_op jit(solution)/shard_map/dot_general | solution.py:20
  275.8 5.0 %fusion.12 = f32[512,227]{0,1:T(8,128)} fusion(bf16[2304,739]{1,0:T(8,128)(2,1)} %bitcast.2, bf16[2304,512]{1,0:T(8,128)(2,1)} %get-tuple-element.29, bf16[512,512]{1,0:T(8,128)(2,1)S(1)} %copy-done), kind=kOutput, calls=%fused_computation.37 | convolution fusion | flops 1744699392 | bytes 4528128 | tf_op jit(solution)/shard_map/dot_general | solution.py:20
  280.9 5.5 %fusion.7 = f32[512,512]{0,1:T(8,128)} fusion(bf16[2304,512]{1,0:T(8,128)(2,1)} %get-tuple-element.27, bf16[2304,512]{1,0:T(8,128)(2,1)} %get-tuple-element.28, bf16[2304,512]{1,0:T(8,128)(2,1)S(1)} %copy-done.4, bf16[2304,739]{1,0:T(8,128)(2,1)} %bitcast.2), kind=kOutput, calls=%fused_computation.29 | convolution fusion | flops 1215037440 | bytes 10485760 | tf_op jit(solution)/shard_map/dot_general | solution.py:20
  286.4 19.2 %reduce-scatter.2.cloned.1.call-done = f32[320,512]{1,0:T(8,128)} async-done(((f32[1280,512]{1,0:T(8,128)}), f32[320,512]{1,0:T(8,128)}) %reduce-scatter.2.cloned.1.call-update) | async-done | bytes 655376 | tf_op jit(solution)/shard_map/reduce_scatter | solution.py:88
  305.7 2.6 convolution_bitcast_fusion
  308.3 1.1 convolution_convert_fusion.3
  309.4 143.7 %all-reduce.3.cloned.1.call-done = (f32[512,512]{0,1:T(8,128)}, f32[512,512]{0,1:T(8,128)}, f32[512,512]{0,1:T(8,128)}, f32[512,227]{0,1:T(8,128)}) async-done(((f32[512,512]{0,1:T(8,128)}, f32[512,512]{0,1:T(8,128)}, f32[512,512]{0,1:T(8,128)}, f32[512,227]{0,1:T(8,128)}), (f32[512,512]{0,1:T(8,128)}, f32[512,512]{0,1:T(8,128)}, f32[512,512]{0,1:T(8,128)}, ...) | async-done | bytes 3610640 | tf_op jit(solution)/shard_map/psum | solution.py:95
  453.1 1.4 broadcast_multiply_fusion.2
  454.5 1.3 copy.29
  455.8 0.8 broadcast_multiply_fusion.3
  456.6 1.3 broadcast_multiply_fusion.1
  458.0 1.3 copy.30
  459.4 1.3 copy.31
  (47 shorter events, 1.6 us)
Async XLA Ops:
  7.2 200.4 %copy-start = (bf16[512,512]{1,0:T(8,128)(2,1)S(1)}, bf16[512,512]{1,0:T(8,128)(2,1)}, u32[]{:S(2)}) copy-start(bf16[512,512]{1,0:T(8,128)(2,1)} %param.16) | copy-start | bytes 1572868
  114.0 7.5 %copy-start.9 = (bf16[512,512]{1,0:T(8,128)(2,1)S(1)}, bf16[512,512]{1,0:T(8,128)(2,1)}, u32[]{:S(2)}) copy-start(bf16[512,512]{1,0:T(8,128)(2,1)} %param.14) | copy-start | bytes 1572868
  114.0 7.5 %copy-start.11 = (bf16[320,512]{1,0:T(8,128)(2,1)S(1)}, bf16[320,512]{1,0:T(8,128)(2,1)}, u32[]{:S(2)}) copy-start(bf16[320,512]{1,0:T(8,128)(2,1)} %param.11) | copy-start | bytes 983044
  114.0 8.6 %copy-start.15 = (s32[3,2304]{1,0:T(4,128)S(1)}, s32[3,2304]{1,0:T(4,128)}, u32[]{:S(2)}) copy-start(s32[3,2304]{1,0:T(4,128)} %param.13) | copy-start | bytes 82948
  114.1 87.5 %all-to-all-start = ((bf16[32,72,739]{2,1,0:T(8,128)(2,1)}), bf16[32,72,739]{2,1,0:T(8,128)(2,1)}, u32[]{:S(2)}, u32[]{:S(2)}) async-start(bf16[32,72,739]{2,1,0:T(8,128)(2,1)} %scatter_fusion), calls=%async_computation | async-start | bytes 7077888 | tf_op jit(solution)/shard_map/all_to_all | solution.py:50
  121.5 35.3 %all-gather.2.cloned.1.call-start = ((), (), s32[]{:S(2)}) async-start(), calls=%async_computation.2 | async-start | bytes 1638400 | tf_op jit(solution)/shard_map/all_gather | solution.py:61
  122.6 183.0 %reduce-scatter.2.cloned.1.call-start = ((), (), s32[]{:S(2)}) async-start(), calls=%async_computation.3 | async-start | bytes 3276800 | tf_op jit(solution)/shard_map/reduce_scatter | solution.py:88
  156.8 9.2 %copy-start.1 = (bf16[1280,512]{1,0:T(8,128)(2,1)S(1)}, bf16[1280,512]{1,0:T(8,128)(2,1)}, u32[]{:S(2)}) copy-start(bf16[1280,512]{1,0:T(8,128)(2,1)} %all-gather.2.cloned.1.call-done) | copy-start | bytes 3932164
  173.5 28.0 %copy-start.14 = (bf16[512,227]{0,1:T(8,128)(2,1)S(1)}, bf16[512,227]{0,1:T(8,128)(2,1)}, u32[]{:S(2)}) copy-start(bf16[512,227]{0,1:T(8,128)(2,1)} %param.17) | copy-start | bytes 697348
  181.0 22.6 %copy-start.16 = (bf16[512,512]{1,0:T(8,128)(2,1)S(1)}, bf16[512,512]{1,0:T(8,128)(2,1)}, u32[]{:S(2)}) copy-start(bf16[512,512]{1,0:T(8,128)(2,1)} %param.15) | copy-start | bytes 1572868
  203.6 4.0 copy-start.5
  203.6 4.0 copy-start.6
  203.6 4.0 copy-start.7
  203.6 4.6 copy-start.8
  269.3 1.5 copy-start.2
  270.8 182.3 %all-reduce.3.cloned.1.call-start = ((), (), s32[]{:S(2)}) async-start(), calls=%async_computation.4 | async-start | bytes 7241728 | tf_op jit(solution)/shard_map/psum | solution.py:95
  275.8 5.0 %copy-start.4 = (bf16[2304,512]{1,0:T(8,128)(2,1)S(1)}, bf16[2304,512]{1,0:T(8,128)(2,1)}, u32[]{:S(2)}) copy-start(bf16[2304,512]{1,0:T(8,128)(2,1)} %get-tuple-element.30) | copy-start | bytes 7077892
  286.4 21.9 %copy-start.10 = (bf16[512,512]{1,0:T(8,128)(2,1)S(1)}, bf16[512,512]{1,0:T(8,128)(2,1)}, u32[]{:S(2)}) copy-start(bf16[512,512]{1,0:T(8,128)(2,1)} %param.14) | copy-start | bytes 1572868
  305.7 2.6 copy-start.3
  453.1 2.7 copy-start.13
  455.8 3.5 copy-start.12
Sparse Core Ops, SparseCore 0:
  124.4 32.3 all-gather.1
  270.9 34.7 reduce-scatter.1
  312.3 140.7 all-reduce.2
where the time goes:
time: 472 us; the launch traced here: 467 us
  waiting for transfers between devices  217 us (46%)
  local copies, waits for them, and re-layouts  134 us (28%)
  other arithmetic  58.8 us (12%)
  matrix products  35.1 us (7%)
  between operations  14 us (3%)
  starting transfers between devices  7.75 us (2%)
    psum x1, waiting for transfers between devices, shards(): mesh_total = lax.psum(mesh_part, ('band', 'sub'))  144 us
    scatter x1, local copies, waits for them, and re-layouts, shards(): jnp.zeros((devices, capacity, row_width), jnp.bfloat16)  102 us
    scatter-add x3, other arithmetic, shards(): node_part.at[local_node[corner]].add(pre_grads[corner].astype(jnp.float32))  51.9 us
    all_gather x1, waiting for transfers between devices, shards(): patch_proj = lax.all_gather(mesh_proj, 'sub', axis=0, tiled=True)  33.9 us
    gather x3, local copies, waits for them, and re-layouts, shards(): patch_proj[local_node[corner]].astype(jnp.float32) + grid_float  24.2 us
    all_to_all x1, waiting for transfers between devices, shards(): lax.all_to_all(send_buffer, ('band', 'sub'), split_axis=0, concat_axis=0,...  20.5 us
    reduce_scatter x1, waiting for transfers between devices, shards(): lax.psum_scatter(node_part, 'sub', scatter_dimension=0, tiled=True)  19.2 us
    dot_general x4, matrix products, contract_rows(): lax.dot_general(left, right, (((0,), (0,)), ((), ())), preferred_element_...  17.9 us
  transfers between devices with their start and end apart: 4, of which 4 were waited for; matrix products, arithmetic and copies ran while one was open for 9% of the time, Pallas kernels for 0%

commit v1 on v0

v1 whole, which is shorter than its diff:
```python
import functools
import math

import jax
import jax.numpy as jnp
from jax import lax
from jax.experimental import pallas as pl
from jax.experimental.pallas import tpu as pltpu
from jax.sharding import PartitionSpec as P

CHUNKS = 3
LANES = 128


def latitude_weight(points, total):
    angle = jnp.pi * ((points.astype(jnp.float32) + 0.5) / total - 0.5)
    return 0.5 * jnp.pi * jnp.cos(angle)


def dot(left, right, left_dim, right_dim):
    return lax.dot_general(
        left, right, (((left_dim,), (right_dim,)), ((), ())), preferred_element_type=jnp.float32
    )


def one_hot(index, dim, size):
    shape = (index.shape[0], size) if dim == 1 else (size, index.shape[1])
    return jnp.where(lax.broadcasted_iota(jnp.int32, shape, dim) == index, 1.0, 0.0).astype(
        jnp.bfloat16
    )


def row_block(rows):
    for block in (256, 128, 64, 32, 16, 8):
        if rows % block == 0:
            return block
    return rows


def pack_body(place, latent, weighted, out, *, block, width, base):
    first = base + pl.program_id(0) * block
    select = one_hot(place[...] - first, 0, block)
    out[:, :width] = dot(select, latent[...], 1, 0).astype(jnp.bfloat16)
    out[:, width:] = dot(select, weighted[...], 1, 1).astype(jnp.bfloat16)


def pack(place, latent, weighted, base, rows):
    width = latent.shape[1]
    extra = weighted.shape[0]
    block = row_block(rows)
    whole = lambda array: pl.BlockSpec(array.shape, lambda i: (0,) * array.ndim)
    return pl.pallas_call(
        functools.partial(pack_body, block=block, width=width, base=base),
        grid=(rows // block,),
        in_specs=[whole(place), whole(latent), whole(weighted)],
        out_specs=pl.BlockSpec((block, width + extra), lambda i: (i, 0)),
        out_shape=jax.ShapeDtypeStruct((rows, width + extra), jnp.bfloat16),
        cost_estimate=pl.CostEstimate(
            flops=2 * rows * latent.shape[0] * (width + extra),
            bytes_accessed=rows * (width + extra) * 4,
            transcendentals=0,
        ),
        name="pack",
    )(place, latent, weighted)


def edge_body(*refs, width, chained):
    rows_in, columns, lanes, table, w_grid, w_both = refs[:6]
    outer, grid_part, node_part = refs[-3:]

    @pl.when(pl.program_id(0) == 0)
    def _():
        if chained:
            for old, new in zip(refs[6:9], refs[-3:]):
                new[...] = old[...]
        else:
            for new in refs[-3:]:
                new[...] = jnp.zeros_like(new)

    latent = rows_in[:, :width]
    weighted = rows_in[:, width:]
    nodes = table.shape[0]
    grid_proj = dot(latent, w_grid[...], 1, 0).astype(jnp.bfloat16).astype(jnp.float32)
    act_grad = dot(weighted, w_both[...], 1, 1)
    act_sum = None
    proj_grad = None
    node_sum = None
    for corner in range(3):
        gathered = dot(one_hot(columns[:, corner : corner + 1], 1, nodes), table[...], 1, 0)
        pre = gathered + grid_proj
        sigma = 0.5 * jnp.tanh(0.5 * pre) + 0.5
        act = pre * sigma
        grad = (act_grad * (sigma + act * (1.0 - sigma))).astype(jnp.bfloat16)
        spread = dot(one_hot(lanes[corner : corner + 1, :], 0, nodes), grad, 1, 0)
        wide = grad.astype(jnp.float32)
        act_sum = act if act_sum is None else act_sum + act
        proj_grad = wide if proj_grad is None else proj_grad + wide
        node_sum = spread if node_sum is None else node_sum + spread
    node_part[...] += node_sum
    outer[...] += dot(weighted, act_sum.astype(jnp.bfloat16), 0, 0)
    grid_part[...] += dot(latent, proj_grad.astype(jnp.bfloat16), 0, 0)


def edges(rows_in, columns, lanes, table, w_grid, w_both, previous):
    rows, row_width = rows_in.shape
    nodes, width = table.shape
    extra = row_width - width
    block = row_block(rows)
    whole = lambda shape: pl.BlockSpec(shape, lambda i: (0,) * len(shape))
    shapes = ((extra, width), (width, width), (nodes, width))
    chained = previous is not None
    in_specs = [
        pl.BlockSpec((block, row_width), lambda i: (i, 0)),
        pl.BlockSpec((block, columns.shape[1]), lambda i: (i, 0)),
        pl.BlockSpec((lanes.shape[0], block), lambda i: (0, i)),
        whole(table.shape),
        whole(w_grid.shape),
        whole(w_both.shape),
    ]
    operands = [rows_in, columns, lanes, table, w_grid, w_both]
    if chained:
        in_specs += [whole(shape) for shape in shapes]
        operands += list(previous)
    return pl.pallas_call(
        functools.partial(edge_body, width=width, chained=chained),
        grid=(rows // block,),
        in_specs=in_specs,
        out_specs=[whole(shape) for shape in shapes],
        out_shape=[jax.ShapeDtypeStruct(shape, jnp.float32) for shape in shapes],
        compiler_params=pltpu.CompilerParams(vmem_limit_bytes=56 * 1024 * 1024),
        cost_estimate=pl.CostEstimate(
            flops=2 * rows * width * (6 * nodes + 2 * width + 2 * extra),
            bytes_accessed=rows * row_width * 2 + 4 * nodes * width * 4,
            transcendentals=3 * rows * width,
        ),
        name="edges",
    )(*operands)


def shards(grad_pred, grid_latent, mesh_latent, send_slot, edge_src, w_mesh, w_grid, w_msg, w_out):
    grid_rows, width = grid_latent.shape
    channels = grad_pred.shape[0]
    axes = ("band", "sub")
    devices = lax.axis_size(axes)
    members = lax.axis_size("sub")
    capacity = 3 * grid_rows // devices
    total_points = grid_rows * devices
    extra = -(-channels // LANES) * LANES
    step = capacity // CHUNKS
    chunk_rows = devices * step

    patch_latent = lax.all_gather(mesh_latent, "sub", axis=0, tiled=True)
    patch_size = patch_latent.shape[0]

    points = lax.axis_index(axes) * grid_rows + jnp.arange(grid_rows, dtype=jnp.int32)
    weighted = (
        latitude_weight(points, total_points)[None, :] * grad_pred.astype(jnp.float32)
    ).astype(jnp.bfloat16)
    weighted = jnp.pad(weighted, ((0, extra - channels), (0, 0)))
    target = send_slot // capacity
    rank = send_slot % capacity
    place = (rank // step) * chunk_rows + target * step + rank % step
    place = place[None, :]
    arrived = []
    for chunk in range(CHUNKS):
        packed = pack(place, grid_latent, weighted, chunk * chunk_rows, chunk_rows)
        received = lax.all_to_all(
            packed.reshape(devices, step, width + extra), axes, split_axis=0, concat_axis=0, tiled=True
        )
        arrived.append(received.reshape(chunk_rows, width + extra))

    local = edge_src - lax.axis_index("band") * patch_size
    local = local.reshape(3, devices, CHUNKS, step).transpose(2, 0, 1, 3)
    local = local.reshape(CHUNKS, 3, chunk_rows)
    local_columns = local.transpose(0, 2, 1)
    w_both = jnp.pad(
        dot(w_msg, w_out, 1, 0).astype(jnp.bfloat16), ((0, 0), (0, extra - channels))
    )
    table = dot(patch_latent, w_mesh, 1, 0).astype(jnp.bfloat16)
    sums = None
    for chunk in range(CHUNKS):
        sums = edges(
            arrived[chunk], local_columns[chunk], local[chunk], table, w_grid, w_both, sums
        )
    outer_part, grid_part, node_part = sums

    node_sent = node_part.astype(jnp.bfloat16)
    mesh_part = dot(patch_latent, node_sent, 0, 0)
    node_blocks = lax.all_to_all(
        node_sent.reshape(members, patch_size // members, width),
        "sub",
        split_axis=0,
        concat_axis=0,
        tiled=True,
    )
    outer_total, grid_total, mesh_total = lax.psum(
        (
            outer_part.astype(jnp.bfloat16),
            grid_part.astype(jnp.bfloat16),
            mesh_part.astype(jnp.bfloat16),
        ),
        axes,
    )
    mesh_proj_grad = jnp.sum(node_blocks.astype(jnp.float32), axis=0).astype(jnp.bfloat16)
    mesh_grad = dot(mesh_proj_grad, w_mesh, 1, 1).astype(jnp.bfloat16)
    grad_scale = 1.0 / math.sqrt(3.0 * total_points)
    outer_total = outer_total[:channels]
    out_total = dot(w_msg, outer_total, 0, 1)
    msg_total = dot(outer_total, w_out, 0, 1)
    return (
        mesh_grad,
        mesh_total.astype(jnp.float32) * grad_scale,
        grid_total.astype(jnp.float32) * grad_scale,
        msg_total * grad_scale,
        out_total * grad_scale,
    )


def solution(mesh):
    placed = (
        P(None, ("band", "sub")),
        P(("band", "sub"), None),
        P(("band", "sub"), None),
        P(("band", "sub")),
        P(None, ("band", "sub")),
        P(),
        P(),
        P(),
        P(),
    )
    return jax.shard_map(
        shards,
        mesh=mesh,
        in_specs=placed,
        out_specs=(P(("band", "sub"), None), P(), P(), P(), P()),
        check_vma=False,
    )
```

time: 472 us -> 296 us (0.63)
  local copies, waits for them, and re-layouts: 134 us -> 6.96 us
  Pallas kernels: 0 us -> 56 us
  other arithmetic: 58.8 us -> 8.51 us
  waiting for transfers between devices: 217 us -> 180 us
  matrix products: 35.1 us -> 11.1 us
  starting transfers between devices: 7.75 us -> 18.4 us
    scatter x1 -> x0, local copies, waits for them, and re-layouts: 102 us -> none  [shards(): jnp.zeros((devices, capacity, row_width), jnp.bfloat16)]
    pallas_call x0 -> x6, Pallas kernels: none -> 56 us  [the longest x3 44.6 us: edges(): pl.pallas_call(functools.partial(edge_body, width=width, chained=chained)...]
    scatter-add x3 -> x0, other arithmetic: 51.9 us -> none  [shards(): node_part.at[local_node[corner]].add(pre_grads[corner].astype(jnp.float32))]
    all_gather x1, waiting for transfers between devices: 33.9 us -> 0.01 us  [shards(): patch_latent = lax.all_gather(mesh_latent, 'sub', axis=0, tiled=True)]
    all_to_all x1 -> x4, waiting for transfers between devices: 20.5 us -> 48.8 us  [the longest x3 48.8 us: shards(): lax.all_to_all(packed.reshape(devices, step, width + extra), axes, split_...]
    gather x3 -> x0, local copies, waits for them, and re-layouts: 24.2 us -> none  [shards(): patch_proj[local_node[corner]].astype(jnp.float32) + grid_float]
    dot_general x9 -> x6, matrix products: 35.1 us -> 11.1 us  [dot(): lax.dot_general(left, right, (((left_dim,), (right_dim,)), ((), ())), pre...]
    reduce_scatter x1 -> x0, waiting for transfers between devices: 19.2 us -> none  [shards(): lax.psum_scatter(node_part, 'sub', scatter_dimension=0, tiled=True)]
  transfers between devices with their start and end apart: 4 -> 6, of which waited for: 4 -> 3; matrix products, arithmetic and copies ran while one was open for 9% -> 5% of each run, Pallas kernels for 0% -> 12%
where the time goes in v1:
time: 296 us; the launch traced here: 295 us
  waiting for transfers between devices  180 us (61%)
  Pallas kernels  56 us (19%)
  starting transfers between devices  18.4 us (6%)
  between operations  14.2 us (5%)
  matrix products  11.1 us (4%)
  other arithmetic  8.51 us (3%)
  local copies, waits for them, and re-layouts  6.96 us (2%)
    psum x1, waiting for transfers between devices, shards(): lax.psum((outer_part.astype(jnp.bfloat16), grid_part.astype(jnp.bfloat16)...  131 us
    all_to_all x3, waiting for transfers between devices, shards(): lax.all_to_all(packed.reshape(devices, step, width + extra), axes, split_...  48.8 us
    pallas_call x3, Pallas kernels, edges(): pl.pallas_call(functools.partial(edge_body, width=width, chained=chained)...  44.6 us
    all_to_all x3, starting transfers between devices, shards(): lax.all_to_all(packed.reshape(devices, step, width + extra), axes, split_...  14.8 us
    pallas_call x3, Pallas kernels, pack(): pl.pallas_call(functools.partial(pack_body, block=block, width=width, bas...  11.4 us
    dot_general x6, matrix products, dot(): lax.dot_general(left, right, (((left_dim,), (right_dim,)), ((), ())), pre...  11.1 us
  transfers between devices with their start and end apart: 6, of which 3 were waited for; matrix products, arithmetic and copies ran while one was open for 5% of the time, Pallas kernels for 12%

profile of v1, /device:TPU:0, one launch (start us, length us, event | category | flops | bytes accessed | tf_op | source)
XLA Modules:
  0.0 295.3 jit_solution(17132404271721044251)
XLA Ops:
  7.2 0.8 fusion.6
  8.6 1.0 multiply_convert_fusion
  9.6 0.8 pad.8.weighted
  10.4 3.8 %pack.5 = bf16[768,768]{1,0:T(8,128)(2,1)} custom-call(s32[1,768]{1,0:T(1,128)} %broadcast_in_dim.4.place, bf16[768,512]{1,0:T(8,128)(2,1)} %latent.5, bf16[256,768]{1,0:T(8,128)(2,1)} %pad.8.weighted), custom_call_target="tpu_custom_call" | custom-call | flops 905969664 | bytes 2359296 | tf_op jit(solution)/shard_map/pack/pallas_call | solution.py:52
  14.2 7.3 %all-to-all-start.2 = ((bf16[32,24,768]{2,1,0:T(8,128)(2,1)}), bf16[32,24,768]{2,1,0:T(8,128)(2,1)S(1)}, u32[]{:S(2)}, u32[]{:S(2)}) async-start(bf16[32,24,768]{2,1,0:T(8,128)(2,1)} %bitcast.37), calls=%async_computation.2 | async-start | bytes 2359296 | tf_op jit(solution)/shard_map/all_to_all | solution.py:167
  21.5 3.8 %pack.4 = bf16[768,768]{1,0:T(8,128)(2,1)} custom-call(s32[1,768]{1,0:T(1,128)} %broadcast_in_dim.4.place, bf16[768,512]{1,0:T(8,128)(2,1)} %latent.5, bf16[256,768]{1,0:T(8,128)(2,1)} %pad.8.weighted), custom_call_target="tpu_custom_call" | custom-call | flops 905969664 | bytes 2359296 | tf_op jit(solution)/shard_map/pack/pallas_call | solution.py:52
  25.3 25.2 %all-to-all-done.2 = bf16[32,24,768]{2,1,0:T(8,128)(2,1)S(1)} async-done(((bf16[32,24,768]{2,1,0:T(8,128)(2,1)}), bf16[32,24,768]{2,1,0:T(8,128)(2,1)S(1)}, u32[]{:S(2)}, u32[]{:S(2)}) %all-to-all-start.2) | async-done | bytes 1179680 | tf_op jit(solution)/shard_map/all_to_all | solution.py:167
  50.5 3.7 %all-to-all-start.1 = ((bf16[32,24,768]{2,1,0:T(8,128)(2,1)}), bf16[32,24,768]{2,1,0:T(8,128)(2,1)}, u32[]{:S(2)}, u32[]{:S(2)}) async-start(bf16[32,24,768]{2,1,0:T(8,128)(2,1)} %bitcast.36), calls=%async_computation.1 | async-start | bytes 2359296 | tf_op jit(solution)/shard_map/all_to_all | solution.py:167
  54.3 0.7 all-gather.2.cloned.1.call-update
  55.2 0.6 copy.21
  55.9 3.8 %pack.3 = bf16[768,768]{1,0:T(8,128)(2,1)} custom-call(s32[1,768]{1,0:T(1,128)} %broadcast_in_dim.4.place, bf16[768,512]{1,0:T(8,128)(2,1)} %latent.5, bf16[256,768]{1,0:T(8,128)(2,1)} %pad.8.weighted), custom_call_target="tpu_custom_call" | custom-call | flops 905969664 | bytes 2359296 | tf_op jit(solution)/shard_map/pack/pallas_call | solution.py:52
  59.7 23.6 %all-to-all-done.1 = bf16[32,24,768]{2,1,0:T(8,128)(2,1)} async-done(((bf16[32,24,768]{2,1,0:T(8,128)(2,1)}), bf16[32,24,768]{2,1,0:T(8,128)(2,1)}, u32[]{:S(2)}, u32[]{:S(2)}) %all-to-all-start.1) | async-done | bytes 1179680 | tf_op jit(solution)/shard_map/all_to_all | solution.py:167
  83.3 3.7 %all-to-all-start = ((bf16[32,24,768]{2,1,0:T(8,128)(2,1)}), bf16[32,24,768]{2,1,0:T(8,128)(2,1)}, u32[]{:S(2)}, u32[]{:S(2)}) async-start(bf16[32,24,768]{2,1,0:T(8,128)(2,1)} %bitcast.35), calls=%async_computation | async-start | bytes 2359296 | tf_op jit(solution)/shard_map/all_to_all | solution.py:167
  87.5 0.7 squeeze.23.refs_2_
  88.7 0.7 pad.9.refs_5_
  89.4 0.7 squeeze.21.refs_2_
  90.1 0.7 squeeze.19.refs_2_
  90.8 1.0 slice_bitcast_fusion
  91.8 3.2 %convolution_convert_fusion.refs_3_ = bf16[1280,512]{1,0:T(8,128)(2,1)} fusion(bf16[1280,512]{1,0:T(8,128)(2,1)} %all-gather.2.cloned.1.call-done, bf16[512,512]{1,0:T(8,128)(2,1)S(1)} %copy-done), kind=kOutput, calls=%fused_computation | convolution fusion | flops 671744000 | bytes 3145728 | tf_op jit(solution)/shard_map/dot_general | solution.py:21
  95.1 14.0 %edges.3 = (f32[256,512]{1,0:T(8,128)}, f32[512,512]{1,0:T(8,128)}, f32[1280,512]{1,0:T(8,128)}) custom-call(bf16[768,768]{1,0:T(8,128)(2,1)} %bitcast.34, s32[768,3]{1,0:T(8,128)} %get-tuple-element.29.refs_1_, s32[3,768]{1,0:T(4,128)} %squeeze.23.refs_2_, bf16[1280,512]{1,0:T(8,128)(2,1)} %convolution_convert_fusion.refs_3_, bf16[512,512]{1,0:T(8,128)(2,1)} %refs_4_.5, ...), custom_call_target="tpu_custom_call" | custom-call | flops 7247757312 | bytes 11665408 | tf_op jit(solution)/shard_map/edges/pallas_call | solution.py:124
  109.0 15.3 %edges.4 = (f32[256,512]{1,0:T(8,128)}, f32[512,512]{1,0:T(8,128)}, f32[1280,512]{1,0:T(8,128)}) custom-call(bf16[768,768]{1,0:T(8,128)(2,1)} %bitcast.7.refs_0_, s32[768,3]{1,0:T(8,128)} %get-tuple-element.30.refs_1_, s32[3,768]{1,0:T(4,128)} %squeeze.21.refs_2_, bf16[1280,512]{1,0:T(8,128)(2,1)} %convolution_convert_fusion.refs_3_, ...), custom_call_target="tpu_custom_call" | custom-call | flops 7247757312 | bytes 11665408 | tf_op jit(solution)/shard_map/edges/pallas_call | solution.py:124
  124.3 15.3 %edges.5 = (f32[256,512]{1,0:T(8,128)}, f32[512,512]{1,0:T(8,128)}, f32[1280,512]{1,0:T(8,128)}) custom-call(bf16[768,768]{1,0:T(8,128)(2,1)} %bitcast.1.refs_0_, s32[768,3]{1,0:T(8,128)} %get-tuple-element.31.refs_1_, s32[3,768]{1,0:T(4,128)} %squeeze.19.refs_2_, bf16[1280,512]{1,0:T(8,128)(2,1)} %convolution_convert_fusion.refs_3_, ...), custom_call_target="tpu_custom_call" | custom-call | flops 7247757312 | bytes 11665408 | tf_op jit(solution)/shard_map/edges/pallas_call | solution.py:124
  139.7 3.1 %convert_element_type.54 = bf16[1280,512]{1,0:T(8,128)(2,1)} convert(f32[1280,512]{1,0:T(8,128)} %get-tuple-element.20) | non-fusion elementwise | flops 655360 | bytes 3932160 | tf_op jit(solution)/shard_map/convert_element_type | solution.py:187
  142.8 0.9 convert_element_type.59
  144.0 0.7 convert_element_type.61
  144.7 3.0 %fusion = bf16[512,512]{1,0:T(8,128)(2,1)} fusion(bf16[1280,512]{1,0:T(8,128)(2,1)} %convert_element_type.54, bf16[1280,512]{1,0:T(8,128)(2,1)S(1)} %copy-done.10), kind=kOutput, calls=%fused_computation.3 | convolution fusion | flops 671350784 | bytes 3145728 | tf_op jit(solution)/shard_map/dot_general | solution.py:21
  147.8 3.6 %all-to-all-start.3 = ((bf16[4,320,512]{2,1,0:T(8,128)(2,1)}), bf16[4,320,512]{2,1,0:T(8,128)(2,1)S(1)}, u32[]{:S(2)}, u32[]{:S(2)}) async-start(bf16[4,320,512]{2,1,0:T(8,128)(2,1)} %bitcast.13), calls=%async_computation.3 | async-start | bytes 2621440 | tf_op jit(solution)/shard_map/all_to_all | solution.py:189
  151.3 130.7 %all-reduce.5.cloned.1.call-done = (bf16[512,512]{1,0:T(8,128)(2,1)}, bf16[512,512]{1,0:T(8,128)(2,1)}, bf16[256,512]{1,0:T(8,128)(2,1)}) async-done(((bf16[512,512]{1,0:T(8,128)(2,1)}, bf16[512,512]{1,0:T(8,128)(2,1)}, bf16[256,512]{1,0:T(8,128)(2,1)}), (bf16[512,512]{1,0:T(8,128)(2,1)}, bf16[512,512]{1,0:T(8,128)(2,1)}, bf16[256,512]{1,0:T(8,128)(2,1)})) %all-reduce.5.cloned.1.call-update) | async-done | bytes 1310736 | tf_op jit(solution)/shard_map/psum | solution.py:196
  282.0 2.1 fusion.1
  284.1 1.3 convolution_multiply_fusion
  285.4 1.6 convert_multiply_fusion
  287.4 1.1 convolution_convert_fusion.2
  (36 shorter events, 2.5 us)
Async XLA Ops:
  7.2 84.7 %copy-start = (bf16[512,512]{1,0:T(8,128)(2,1)S(1)}, bf16[512,512]{1,0:T(8,128)(2,1)}, u32[]{:S(2)}) copy-start(bf16[512,512]{1,0:T(8,128)(2,1)} %param.14) | copy-start | bytes 1572868
  14.2 36.3 %all-to-all-start.2 = ((bf16[32,24,768]{2,1,0:T(8,128)(2,1)}), bf16[32,24,768]{2,1,0:T(8,128)(2,1)S(1)}, u32[]{:S(2)}, u32[]{:S(2)}) async-start(bf16[32,24,768]{2,1,0:T(8,128)(2,1)} %bitcast.37), calls=%async_computation.2 | async-start | bytes 2359296 | tf_op jit(solution)/shard_map/all_to_all | solution.py:167
  50.5 4.5 %copy-start.2 = (bf16[32,24,768]{2,1,0:T(8,128)(2,1)}, bf16[32,24,768]{2,1,0:T(8,128)(2,1)S(1)}, u32[]{:S(2)}) copy-start(bf16[32,24,768]{2,1,0:T(8,128)(2,1)S(1)} %all-to-all-done.2) | copy-start | bytes 3538948
  50.5 4.5 %copy-start.9 = (s32[3,2304]{1,0:T(4,128)S(1)}, s32[3,2304]{1,0:T(4,128)}, u32[]{:S(2)}) copy-start(s32[3,2304]{1,0:T(4,128)} %param.13) | copy-start | bytes 82948
  50.5 32.7 %all-to-all-start.1 = ((bf16[32,24,768]{2,1,0:T(8,128)(2,1)}), bf16[32,24,768]{2,1,0:T(8,128)(2,1)}, u32[]{:S(2)}, u32[]{:S(2)}) async-start(bf16[32,24,768]{2,1,0:T(8,128)(2,1)} %bitcast.36), calls=%async_computation.1 | async-start | bytes 2359296 | tf_op jit(solution)/shard_map/all_to_all | solution.py:167
  54.3 37.6 %all-gather.2.cloned.1.call-start = ((), (), s32[]{:S(2)}) async-start(), calls=%async_computation.4 | async-start | bytes 1638400 | tf_op jit(solution)/shard_map/all_gather | solution.py:152
  83.3 4.9 %copy-start.1 = (bf16[512,512]{1,0:T(8,128)(2,1)S(1)}, bf16[512,512]{1,0:T(8,128)(2,1)}, u32[]{:S(2)}) copy-start(bf16[512,512]{1,0:T(8,128)(2,1)} %param.16) | copy-start | bytes 1572868
  83.3 4.9 %copy-start.4 = (bf16[512,227]{0,1:T(8,128)(2,1)S(1)}, bf16[512,227]{0,1:T(8,128)(2,1)}, u32[]{:S(2)}) copy-start(bf16[512,227]{0,1:T(8,128)(2,1)} %param.17) | copy-start | bytes 697348
  83.3 41.1 %all-to-all-start = ((bf16[32,24,768]{2,1,0:T(8,128)(2,1)}), bf16[32,24,768]{2,1,0:T(8,128)(2,1)}, u32[]{:S(2)}, u32[]{:S(2)}) async-start(bf16[32,24,768]{2,1,0:T(8,128)(2,1)} %bitcast.35), calls=%async_computation | async-start | bytes 2359296 | tf_op jit(solution)/shard_map/all_to_all | solution.py:167
  87.0 195.0 %all-reduce.5.cloned.1.call-start = ((), (), s32[]{:S(2)}) async-start(), calls=%async_computation.5 | async-start | bytes 2621440 | tf_op jit(solution)/shard_map/psum | solution.py:196
  139.7 3.1 %copy-start.3 = (f32[512,512]{1,0:T(8,128)S(1)}, f32[512,512]{1,0:T(8,128)}, u32[]{:S(2)}) copy-start(f32[512,512]{1,0:T(8,128)} %get-tuple-element.21) | copy-start | bytes 3145732
  142.8 1.2 copy-start.6
  142.8 1.9 copy-start.10
  147.8 139.3 %all-to-all-start.3 = ((bf16[4,320,512]{2,1,0:T(8,128)(2,1)}), bf16[4,320,512]{2,1,0:T(8,128)(2,1)S(1)}, u32[]{:S(2)}, u32[]{:S(2)}) async-start(bf16[4,320,512]{2,1,0:T(8,128)(2,1)} %bitcast.13), calls=%async_computation.3 | async-start | bytes 2621440 | tf_op jit(solution)/shard_map/all_to_all | solution.py:189
  282.0 2.1 copy-start.5
  282.0 3.4 %copy-start.7 = (bf16[512,512]{1,0:T(8,128)(2,1)S(1)}, bf16[512,512]{1,0:T(8,128)(2,1)}, u32[]{:S(2)}) copy-start(bf16[512,512]{1,0:T(8,128)(2,1)} %get-tuple-element.26) | copy-start | bytes 1572868
  282.0 3.4 %copy-start.8 = (bf16[512,512]{1,0:T(8,128)(2,1)S(1)}, bf16[512,512]{1,0:T(8,128)(2,1)}, u32[]{:S(2)}) copy-start(bf16[512,512]{1,0:T(8,128)(2,1)} %get-tuple-element.27) | copy-start | bytes 1572868
Sparse Core Ops, SparseCore 0:
  56.6 22.2 all-gather.1
  147.9 134.0 all-reduce.4

commit v2 on v1

--- a/solution.py
+++ b/solution.py
@@ -37,22 +37,28 @@
     return rows
 
 
-def pack_body(place, latent, weighted, out, *, block, width, base):
+def pack_body(place, latent, weighted, *rest, block, width, base):
+    out = rest[-1]
     first = base + pl.program_id(0) * block
     select = one_hot(place[...] - first, 0, block)
     out[:, :width] = dot(select, latent[...], 1, 0).astype(jnp.bfloat16)
     out[:, width:] = dot(select, weighted[...], 1, 1).astype(jnp.bfloat16)
 
 
-def pack(place, latent, weighted, base, rows):
+def pack(place, latent, weighted, base, rows, after):
     width = latent.shape[1]
     extra = weighted.shape[0]
     block = row_block(rows)
     whole = lambda array: pl.BlockSpec(array.shape, lambda i: (0,) * array.ndim)
+    in_specs = [whole(place), whole(latent), whole(weighted)]
+    operands = [place, latent, weighted]
+    if after is not None:
+        in_specs.append(pl.BlockSpec((8, LANES), lambda i: (0, 0)))
+        operands.append(after)
     return pl.pallas_call(
         functools.partial(pack_body, block=block, width=width, base=base),
         grid=(rows // block,),
-        in_specs=[whole(place), whole(latent), whole(weighted)],
+        in_specs=in_specs,
         out_specs=pl.BlockSpec((block, width + extra), lambda i: (i, 0)),
         out_shape=jax.ShapeDtypeStruct((rows, width + extra), jnp.bfloat16),
         cost_estimate=pl.CostEstimate(
@@ -61,20 +67,21 @@
             transcendentals=0,
         ),
         name="pack",
-    )(place, latent, weighted)
-
-
-def edge_body(*refs, width, chained):
+    )(*operands)
+
+
+def edge_body(*refs, width, chained, last):
     rows_in, columns, lanes, table, w_grid, w_both = refs[:6]
-    outer, grid_part, node_part = refs[-3:]
+    sums = refs[-3:]
+    outer, grid_part, node_part = sums
 
     @pl.when(pl.program_id(0) == 0)
     def _():
         if chained:
-            for old, new in zip(refs[6:9], refs[-3:]):
+            for old, new in zip(refs[6:9], sums):
                 new[...] = old[...]
         else:
-            for new in refs[-3:]:
+            for new in sums:
                 new[...] = jnp.zeros_like(new)
 
     latent = rows_in[:, :width]
@@ -100,8 +107,20 @@
     outer[...] += dot(weighted, act_sum.astype(jnp.bfloat16), 0, 0)
     grid_part[...] += dot(latent, proj_grad.astype(jnp.bfloat16), 0, 0)
 
-
-def edges(rows_in, columns, lanes, table, w_grid, w_both, previous):
+    if last:
+        patch_latent, stack, node_sent = refs[9:12]
+        extra = outer.shape[0]
+
+        @pl.when(pl.program_id(0) == pl.num_programs(0) - 1)
+        def _():
+            node_sent[...] = node_part[...].astype(jnp.bfloat16)
+            stack[:extra, :] = outer[...].astype(jnp.bfloat16)
+            stack[extra : extra + width, :] = grid_part[...].astype(jnp.bfloat16)
+            mesh_part = dot(patch_latent[...], node_sent[...], 0, 0)
+            stack[extra + width :, :] = mesh_part.astype(jnp.bfloat16)
+
+
+def edges(rows_in, columns, lanes, table, w_grid, w_both, previous, patch_latent):
     rows, row_width = rows_in.shape
     nodes, width = table.shape
     extra = row_width - width
@@ -109,6 +128,7 @@
     whole = lambda shape: pl.BlockSpec(shape, lambda i: (0,) * len(shape))
     shapes = ((extra, width), (width, width), (nodes, width))
     chained = previous is not None
+    last = patch_latent is not None
     in_specs = [
         pl.BlockSpec((block, row_width), lambda i: (i, 0)),
         pl.BlockSpec((block, columns.shape[1]), lambda i: (i, 0)),
@@ -121,12 +141,23 @@
     if chained:
         in_specs += [whole(shape) for shape in shapes]
         operands += list(previous)
+    out_shape = [jax.ShapeDtypeStruct(shape, jnp.float32) for shape in shapes]
+    scratch = []
+    if last:
+        in_specs.append(whole(patch_latent.shape))
+        operands.append(patch_latent)
+        out_shape = [
+            jax.ShapeDtypeStruct(shape, jnp.bfloat16)
+            for shape in ((extra + 2 * width, width), (nodes, width))
+        ]
+        scratch = [pltpu.VMEM(shape, jnp.float32) for shape in shapes]
     return pl.pallas_call(
-        functools.partial(edge_body, width=width, chained=chained),
+        functools.partial(edge_body, width=width, chained=chained, last=last),
         grid=(rows // block,),
         in_specs=in_specs,
-        out_specs=[whole(shape) for shape in shapes],
-        out_shape=[jax.ShapeDtypeStruct(shape, jnp.float32) for shape in shapes],
+        out_specs=[whole(out.shape) for out in out_shape],
+        out_shape=out_shape,
+        scratch_shapes=scratch,
         compiler_params=pltpu.CompilerParams(vmem_limit_bytes=56 * 1024 * 1024),
         cost_estimate=pl.CostEstimate(
             flops=2 * rows * width * (6 * nodes + 2 * width + 2 * extra),
@@ -137,20 +168,54 @@
     )(*operands)
 
 
+def total_body(parts, out):
+    total = parts[0].astype(jnp.float32)
+    for part in range(1, parts.shape[0]):
+        total = total + parts[part].astype(jnp.float32)
+    total = total.astype(jnp.bfloat16)
+    for part in range(parts.shape[0]):
+        out[part] = total
+
+
+def total_for_all(parts):
+    return pl.pallas_call(
+        total_body, out_shape=jax.ShapeDtypeStruct(parts.shape, parts.dtype), name="total"
+    )(parts)
+
+
 def shards(grad_pred, grid_latent, mesh_latent, send_slot, edge_src, w_mesh, w_grid, w_msg, w_out):
     grid_rows, width = grid_latent.shape
+    mesh_rows = mesh_latent.shape[0]
     channels = grad_pred.shape[0]
     axes = ("band", "sub")
     devices = lax.axis_size(axes)
     members = lax.axis_size("sub")
     capacity = 3 * grid_rows // devices
     total_points = grid_rows * devices
+    patch_size = members * mesh_rows
     extra = -(-channels // LANES) * LANES
     step = capacity // CHUNKS
     chunk_rows = devices * step
 
-    patch_latent = lax.all_gather(mesh_latent, "sub", axis=0, tiled=True)
-    patch_size = patch_latent.shape[0]
+    def exchange(blocks):
+        return lax.all_to_all(blocks, axes, split_axis=0, concat_axis=0, tiled=True)
+
+    def from_member(block, shift):
+        pairs = [((to + shift) % members, to) for to in range(members)]
+        return lax.ppermute(block, "sub", pairs)
+
+    patch_latent = jnp.concatenate(
+        [mesh_latent] + [from_member(mesh_latent, shift) for shift in range(1, members)]
+    )
+    first_node = lax.axis_index(axes) * mesh_rows
+    local = (edge_src - first_node) % patch_size
+    local = local.reshape(3, devices, CHUNKS, step).transpose(2, 0, 1, 3)
+    local = local.reshape(CHUNKS, 3, chunk_rows)
+    local_columns = local.transpose(0, 2, 1)
+    w_both = jnp.pad(
+        dot(w_msg, w_out, 1, 0).astype(jnp.bfloat16), ((0, 0), (0, extra - channels))
+    )
+    table = dot(patch_latent, w_mesh, 1, 0).astype(jnp.bfloat16)
 
     points = lax.axis_index(axes) * grid_rows + jnp.arange(grid_rows, dtype=jnp.int32)
     weighted = (
@@ -161,56 +226,45 @@
     rank = send_slot % capacity
     place = (rank // step) * chunk_rows + target * step + rank % step
     place = place[None, :]
-    arrived = []
-    for chunk in range(CHUNKS):
-        packed = pack(place, grid_latent, weighted, chunk * chunk_rows, chunk_rows)
-        received = lax.all_to_all(
-            packed.reshape(devices, step, width + extra), axes, split_axis=0, concat_axis=0, tiled=True
-        )
-        arrived.append(received.reshape(chunk_rows, width + extra))
-
-    local = edge_src - lax.axis_index("band") * patch_size
-    local = local.reshape(3, devices, CHUNKS, step).transpose(2, 0, 1, 3)
-    local = local.reshape(CHUNKS, 3, chunk_rows)
-    local_columns = local.transpose(0, 2, 1)
-    w_both = jnp.pad(
-        dot(w_msg, w_out, 1, 0).astype(jnp.bfloat16), ((0, 0), (0, extra - channels))
-    )
-    table = dot(patch_latent, w_mesh, 1, 0).astype(jnp.bfloat16)
+
+    def send(chunk, after):
+        packed = pack(place, grid_latent, weighted, chunk * chunk_rows, chunk_rows, after)
+        arrived = exchange(packed.reshape(devices, step, width + extra))
+        return arrived.reshape(chunk_rows, width + extra)
+
+    arrived = [send(chunk, None) for chunk in range(min(2, CHUNKS))]
     sums = None
     for chunk in range(CHUNKS):
         sums = edges(
-            arrived[chunk], local_columns[chunk], local[chunk], table, w_grid, w_both, sums
+            arrived[chunk],
+            local_columns[chunk],
+            local[chunk],
+            table,
+            w_grid,
+            w_both,
+            sums,
+            patch_latent if chunk == CHUNKS - 1 else None,
         )
-    outer_part, grid_part, node_part = sums
-
-    node_sent = node_part.astype(jnp.bfloat16)
-    mesh_part = dot(patch_latent, node_sent, 0, 0)
-    node_blocks = lax.all_to_all(
-        node_sent.reshape(members, patch_size // members, width),
-        "sub",
-        split_axis=0,
-        concat_axis=0,
-        tiled=True,
-    )
-    outer_total, grid_total, mesh_total = lax.psum(
-        (
-            outer_part.astype(jnp.bfloat16),
-            grid_part.astype(jnp.bfloat16),
-            mesh_part.astype(jnp.bfloat16),
-        ),
-        axes,
-    )
-    mesh_proj_grad = jnp.sum(node_blocks.astype(jnp.float32), axis=0).astype(jnp.bfloat16)
+        if chunk + 2 < CHUNKS:
+            arrived.append(send(chunk + 2, sums[0]))
+    stack, node_sent = sums
+
+    shares = exchange(stack.reshape(devices, stack.shape[0] // devices, width))
+    node_blocks = node_sent.reshape(members, mesh_rows, width)
+    node_total = node_blocks[0].astype(jnp.float32)
+    for shift in range(1, members):
+        node_total = node_total + from_member(node_blocks[shift], -shift).astype(jnp.float32)
+    mesh_proj_grad = node_total.astype(jnp.bfloat16)
     mesh_grad = dot(mesh_proj_grad, w_mesh, 1, 1).astype(jnp.bfloat16)
+    totals = exchange(total_for_all(shares)).reshape(stack.shape)
     grad_scale = 1.0 / math.sqrt(3.0 * total_points)
-    outer_total = outer_total[:channels]
+    outer_total = totals[:channels]
     out_total = dot(w_msg, outer_total, 0, 1)
     msg_total = dot(outer_total, w_out, 0, 1)
     return (
         mesh_grad,
-        mesh_total.astype(jnp.float32) * grad_scale,
-        grid_total.astype(jnp.float32) * grad_scale,
+        totals[extra + width :].astype(jnp.float32) * grad_scale,
+        totals[extra : extra + width].astype(jnp.float32) * grad_scale,
         msg_total * grad_scale,
         out_total * grad_scale,
     )

time: 296 us -> 207 us (0.70)
  waiting for transfers between devices: 180 us -> 63.7 us
  blocking collectives: 0 us -> 36.9 us
  between operations: 14.2 us -> 0.84 us
  other arithmetic: 8.51 us -> 3.52 us
  starting transfers between devices: 18.4 us -> 23.3 us
  local copies, waits for them, and re-layouts: 6.96 us -> 11.4 us
  matrix products: 11.1 us -> 6.71 us
  Pallas kernels: 56 us -> 59.3 us
    psum x1 -> x0, waiting for transfers between devices: 131 us -> none  [shards(): lax.psum((outer_part.astype(jnp.bfloat16), grid_part.astype(jnp.bfloat16)...]
    all_to_all x0 -> x1, blocking collectives: none -> 36.9 us  [exchange(): return lax.all_to_all(blocks, axes, split_axis=0, concat_axis=0, tiled=True)]
    ppermute x0 -> x6, waiting for transfers between devices: none -> 26.1 us  [from_member(): return lax.ppermute(block, 'sub', pairs)]
    all_to_all x4, waiting for transfers between devices: 48.8 us -> 37.5 us  [exchange(): return lax.all_to_all(blocks, axes, split_axis=0, concat_axis=0, tiled=True)]
    ppermute x0 -> x6, starting transfers between devices: none -> 5.79 us  [from_member(): return lax.ppermute(block, 'sub', pairs)]
    convert_element_type x3 -> x0, other arithmetic: 4.68 us -> none  [the longest x1 3.09 us: shards(): node_sent = node_part.astype(jnp.bfloat16)]
    dot_general x6 -> x5, matrix products: 11.1 us -> 6.71 us  [dot(): lax.dot_general(left, right, (((left_dim,), (right_dim,)), ((), ())), pre...]
    pallas_call x3 -> x4, Pallas kernels: 44.6 us -> 48 us  [the longest x3 45.4 us: edges(): pl.pallas_call(functools.partial(edge_body, width=width, chained=chained,...]
  transfers between devices with their start and end apart: 6 -> 10, of which waited for: 3 -> 6; matrix products, arithmetic and copies ran while one was open for 5% -> 6% of each run, Pallas kernels for 12% -> 18%
where the time goes in v2:
time: 207 us; the launch traced here: 206 us
  waiting for transfers between devices  63.7 us (31%)
  Pallas kernels  59.3 us (29%)
  blocking collectives  36.9 us (18%)
  starting transfers between devices  23.3 us (11%)
  local copies, waits for them, and re-layouts  11.4 us (6%)
  matrix products  6.71 us (3%)
  other arithmetic  3.52 us (2%)
    pallas_call x3, Pallas kernels, edges(): pl.pallas_call(functools.partial(edge_body, width=width, chained=chained,...  45.4 us
    all_to_all x4, waiting for transfers between devices, exchange(): return lax.all_to_all(blocks, axes, split_axis=0, concat_axis=0, tiled=True)  37.5 us
    all_to_all x1, blocking collectives, exchange(): return lax.all_to_all(blocks, axes, split_axis=0, concat_axis=0, tiled=True)  36.9 us
    ppermute x6, waiting for transfers between devices, from_member(): return lax.ppermute(block, 'sub', pairs)  26.1 us
    all_to_all x4, starting transfers between devices, exchange(): return lax.all_to_all(blocks, axes, split_axis=0, concat_axis=0, tiled=True)  17.5 us
    pallas_call x3, Pallas kernels, pack(): pl.pallas_call(functools.partial(pack_body, block=block, width=width, bas...  11.3 us
    dot_general x5, matrix products, dot(): lax.dot_general(left, right, (((left_dim,), (right_dim,)), ((), ())), pre...  6.71 us
    ppermute x6, starting transfers between devices, from_member(): return lax.ppermute(block, 'sub', pairs)  5.79 us
  transfers between devices with their start and end apart: 10, of which 6 were waited for; matrix products, arithmetic and copies ran while one was open for 6% of the time, Pallas kernels for 18%

profile of v2, /device:TPU:0, one launch (start us, length us, event | category | flops | bytes accessed | tf_op | source)
XLA Modules:
  0.0 205.7 jit_solution(380741630081330258)
XLA Ops:
  2.1 1.0 multiply_convert_fusion
  3.1 0.8 pad.8.weighted
  3.9 3.7 %pack.3 = bf16[768,768]{1,0:T(8,128)(2,1)} custom-call(s32[1,768]{1,0:T(1,128)} %broadcast_in_dim.4.place, bf16[768,512]{1,0:T(8,128)(2,1)} %latent.5, bf16[256,768]{1,0:T(8,128)(2,1)} %pad.8.weighted), custom_call_target="tpu_custom_call" | custom-call | flops 905969664 | bytes 2359296 | tf_op jit(solution)/shard_map/pack/pallas_call | solution.py:58
  7.6 7.3 %all-to-all-start = ((bf16[32,24,768]{2,1,0:T(8,128)(2,1)}), bf16[32,24,768]{2,1,0:T(8,128)(2,1)S(1)}, u32[]{:S(2)}, u32[]{:S(2)}) async-start(bf16[32,24,768]{2,1,0:T(8,128)(2,1)} %bitcast.38), calls=%async_computation | async-start | bytes 2359296 | tf_op jit(solution)/shard_map/all_to_all | solution.py:201
  15.0 1.8 collective-permute-start.1
  17.3 3.8 %pack.5 = bf16[768,768]{1,0:T(8,128)(2,1)} custom-call(s32[1,768]{1,0:T(1,128)} %broadcast_in_dim.4.place, bf16[768,512]{1,0:T(8,128)(2,1)} %latent.5, bf16[256,768]{1,0:T(8,128)(2,1)} %pad.8.weighted), custom_call_target="tpu_custom_call" | custom-call | flops 905969664 | bytes 2359296 | tf_op jit(solution)/shard_map/pack/pallas_call | solution.py:58
  21.1 22.9 %all-to-all-done = bf16[32,24,768]{2,1,0:T(8,128)(2,1)S(1)} async-done(((bf16[32,24,768]{2,1,0:T(8,128)(2,1)}), bf16[32,24,768]{2,1,0:T(8,128)(2,1)S(1)}, u32[]{:S(2)}, u32[]{:S(2)}) %all-to-all-start) | async-done | bytes 1179680 | tf_op jit(solution)/shard_map/all_to_all | solution.py:201
  44.0 3.7 %all-to-all-start.2 = ((bf16[32,24,768]{2,1,0:T(8,128)(2,1)}), bf16[32,24,768]{2,1,0:T(8,128)(2,1)}, u32[]{:S(2)}, u32[]{:S(2)}) async-start(bf16[32,24,768]{2,1,0:T(8,128)(2,1)} %bitcast.35), calls=%async_computation.2 | async-start | bytes 2359296 | tf_op jit(solution)/shard_map/all_to_all | solution.py:201
  48.6 1.0 slice_bitcast_fusion
  52.5 1.0 constant_dynamic-update-slice_fusion.2
  53.5 1.0 constant_dynamic-update-slice_fusion.refs_9_
  54.6 2.0 convolution_convert_fusion.refs_3_
  56.5 14.0 %edges.3 = (f32[256,512]{1,0:T(8,128)}, f32[512,512]{1,0:T(8,128)}, f32[1280,512]{1,0:T(8,128)}) custom-call(bf16[768,768]{1,0:T(8,128)(2,1)} %bitcast.34, s32[768,3]{1,0:T(8,128)} %get-tuple-element.31.refs_1_, s32[3,768]{1,0:T(4,128)} %squeeze.23.refs_2_, bf16[1280,512]{1,0:T(8,128)(2,1)} %convolution_convert_fusion.refs_3_, bf16[512,512]{1,0:T(8,128)(2,1)} %refs_4_.5, ...), custom_call_target="tpu_custom_call" | custom-call | flops 7247757312 | bytes 11665408 | tf_op jit(solution)/shard_map/edges/pallas_call | solution.py:154
  70.5 3.7 %pack.4 = bf16[768,768]{1,0:T(8,128)(2,1)} custom-call(s32[1,768]{1,0:T(1,128)} %broadcast_in_dim.4.place, bf16[768,512]{1,0:T(8,128)(2,1)} %latent.5, bf16[256,768]{1,0:T(8,128)(2,1)} %pad.8.weighted, f32[256,512]{1,0:T(8,128)} %get-tuple-element.13.rest_0_.refs_6_), custom_call_target="tpu_custom_call" | custom-call | flops 905969664 | bytes 2359296 | tf_op jit(solution)/shard_map/pack/pallas_call | solution.py:58
  74.2 2.5 %all-to-all-done.2 = bf16[32,24,768]{2,1,0:T(8,128)(2,1)} async-done(((bf16[32,24,768]{2,1,0:T(8,128)(2,1)}), bf16[32,24,768]{2,1,0:T(8,128)(2,1)}, u32[]{:S(2)}, u32[]{:S(2)}) %all-to-all-start.2) | async-done | bytes 1179680 | tf_op jit(solution)/shard_map/all_to_all | solution.py:201
  76.7 3.8 %all-to-all-start.1 = ((bf16[32,24,768]{2,1,0:T(8,128)(2,1)}), bf16[32,24,768]{2,1,0:T(8,128)(2,1)S(1)}, u32[]{:S(2)}, u32[]{:S(2)}) async-start(bf16[32,24,768]{2,1,0:T(8,128)(2,1)} %bitcast.37), calls=%async_computation.1 | async-start | bytes 2359296 | tf_op jit(solution)/shard_map/all_to_all | solution.py:201
  81.9 15.3 %edges.4 = (f32[256,512]{1,0:T(8,128)}, f32[512,512]{1,0:T(8,128)}, f32[1280,512]{1,0:T(8,128)}) custom-call(bf16[768,768]{1,0:T(8,128)(2,1)} %bitcast.11.refs_0_, s32[768,3]{1,0:T(8,128)} %get-tuple-element.29.refs_1_, s32[3,768]{1,0:T(4,128)} %squeeze.27.refs_2_, bf16[1280,512]{1,0:T(8,128)(2,1)} %convolution_convert_fusion.refs_3_, ...), custom_call_target="tpu_custom_call" | custom-call | flops 7247757312 | bytes 11665408 | tf_op jit(solution)/shard_map/edges/pallas_call | solution.py:154
  97.2 12.2 %all-to-all-done.1 = bf16[32,24,768]{2,1,0:T(8,128)(2,1)S(1)} async-done(((bf16[32,24,768]{2,1,0:T(8,128)(2,1)}), bf16[32,24,768]{2,1,0:T(8,128)(2,1)S(1)}, u32[]{:S(2)}, u32[]{:S(2)}) %all-to-all-start.1) | async-done | bytes 1179680 | tf_op jit(solution)/shard_map/all_to_all | solution.py:201
  109.4 1.1 copy-done.3
  110.4 16.2 %edges.5 = (bf16[1280,512]{1,0:T(8,128)(2,1)}, bf16[1280,512]{1,0:T(8,128)(2,1)}) custom-call(bf16[768,768]{1,0:T(8,128)(2,1)} %bitcast.36, s32[768,3]{1,0:T(8,128)} %get-tuple-element.30.refs_1_, s32[3,768]{1,0:T(4,128)} %squeeze.25.refs_2_, bf16[1280,512]{1,0:T(8,128)(2,1)} %convolution_convert_fusion.refs_3_, bf16[512,512]{1,0:T(8,128)(2,1)} %refs_4_.5, ...), custom_call_target="tpu_custom_call" | custom-call | flops 7247757312 | bytes 11665408 | tf_op jit(solution)/shard_map/edges/pallas_call | solution.py:154
  126.6 36.9 %all_to_all.25.parts = bf16[32,40,512]{2,1,0:T(8,128)(2,1)} all-to-all(bf16[32,40,512]{2,1,0:T(8,128)(2,1)} %bitcast.33), channel_id=1, replica_groups=mesh['band'=8,'sub'=4] {'band','sub'}, dimensions={0} | all-to-all | bytes 2621440 | tf_op jit(solution)/shard_map/all_to_all | solution.py:201
  163.6 2.6 %total.1 = bf16[32,40,512]{2,1,0:T(8,128)(2,1)} custom-call(bf16[32,40,512]{2,1,0:T(8,128)(2,1)} %all_to_all.25.parts), custom_call_target="tpu_custom_call" | custom-call | tf_op jit(solution)/shard_map/total/pallas_call | solution.py:181
  166.2 2.7 %all-to-all-start.4 = ((bf16[32,40,512]{2,1,0:T(8,128)(2,1)}), bf16[32,40,512]{2,1,0:T(8,128)(2,1)S(1)}, u32[]{:S(2)}, u32[]{:S(2)}) async-start(bf16[32,40,512]{2,1,0:T(8,128)(2,1)} %total.1), calls=%async_computation.4 | async-start | bytes 2621440 | tf_op jit(solution)/shard_map/all_to_all | solution.py:201
  168.8 1.2 fusion.10
  170.2 1.6 collective-permute-start.5
  171.9 1.7 collective-permute-start.4
  173.5 15.7 %collective-permute-done.3 = bf16[320,512]{1,0:T(8,128)(2,1)S(1)} collective-permute-done((bf16[320,512]{1,0:T(8,128)(2,1)S(1)}, bf16[320,512]{1,0:T(8,128)(2,1)S(1)}, u32[]{:S(2)}, u32[]{:S(2)}) %collective-permute-start.3) | collective-permute-done | bytes 327712 | tf_op jit(solution)/shard_map/ppermute | solution.py:205
  189.7 9.9 %collective-permute-done.4 = bf16[320,512]{1,0:T(8,128)(2,1)S(1)} collective-permute-done((bf16[320,512]{1,0:T(8,128)(2,1)S(1)}, bf16[320,512]{1,0:T(8,128)(2,1)S(1)}, u32[]{:S(2)}, u32[]{:S(2)}) %collective-permute-start.4) | collective-permute-done | bytes 327712 | tf_op jit(solution)/shard_map/ppermute | solution.py:205
  199.6 2.1 %convolution_convert_fusion.1 = bf16[320,512]{1,0:T(8,128)(2,1)} fusion(bf16[512,512]{1,0:T(8,128)(2,1)S(1)} %copy-done, bf16[320,512]{1,0:T(8,128)(2,1)S(1)} %collective-permute-done.5, bf16[320,512]{1,0:T(8,128)(2,1)S(1)} %collective-permute-done.4, bf16[320,512]{1,0:T(8,128)(2,1)S(1)} %collective-permute-done.3, bf16[1280,512]{1,0:T(8,128)(2,1)} %get-tuple-element.19), kind=kOutput, calls=%fused_computation.2 | convolution fusion | flops 169246720 | bytes 2162688 | tf_op jit(solution)/shard_map/dot_general | solution.py:21
  201.7 1.1 fusion
  202.8 1.3 convolution_multiply_fusion
  204.1 1.6 convert_multiply_fusion
  (38 shorter events, 7.6 us)
Async XLA Ops:
  0.6 53.9 %copy-start = (bf16[512,512]{1,0:T(8,128)(2,1)S(1)}, bf16[512,512]{1,0:T(8,128)(2,1)}, u32[]{:S(2)}) copy-start(bf16[512,512]{1,0:T(8,128)(2,1)} %param.14) | copy-start | bytes 1572868
  7.6 7.3 %copy-start.5 = (bf16[320,512]{1,0:T(8,128)(2,1)S(1)}, bf16[320,512]{1,0:T(8,128)(2,1)}, u32[]{:S(2)}) copy-start(bf16[320,512]{1,0:T(8,128)(2,1)} %param.11) | copy-start | bytes 983044
  7.6 36.3 %all-to-all-start = ((bf16[32,24,768]{2,1,0:T(8,128)(2,1)}), bf16[32,24,768]{2,1,0:T(8,128)(2,1)S(1)}, u32[]{:S(2)}, u32[]{:S(2)}) async-start(bf16[32,24,768]{2,1,0:T(8,128)(2,1)} %bitcast.38), calls=%async_computation | async-start | bytes 2359296 | tf_op jit(solution)/shard_map/all_to_all | solution.py:201
  15.0 38.5 %collective-permute-start.1 = (bf16[320,512]{1,0:T(8,128)(2,1)S(1)}, bf16[320,512]{1,0:T(8,128)(2,1)S(1)}, u32[]{:S(2)}, u32[]{:S(2)}) collective-permute-start(bf16[320,512]{1,0:T(8,128)(2,1)S(1)} %copy-done.5), channel_id=1, source_target_pairs={{2,0},{3,1},{0,2},{1,3},{6,4},{7,5},{4,6},{5,7},{10,8},{11,9},{8,1... | collective-permute-start | bytes 983048 | tf_op jit(solution)/shard_map/ppermute | solution.py:205
  16.8 35.7 %collective-permute-start = (bf16[320,512]{1,0:T(8,128)(2,1)S(1)}, bf16[320,512]{1,0:T(8,128)(2,1)}, u32[]{:S(2)}, u32[]{:S(2)}) collective-permute-start(bf16[320,512]{1,0:T(8,128)(2,1)S(1)} %copy-done.5), channel_id=1, source_target_pairs={{1,0},{2,1},{3,2},{0,3},{5,4},{6,5},{7,6},{4,7},{9,8},{10,9},{11,1... | collective-permute-start | bytes 983048 | tf_op jit(solution)/shard_map/ppermute | solution.py:205
  16.8 36.7 %collective-permute-start.2 = (bf16[320,512]{1,0:T(8,128)(2,1)S(1)}, bf16[320,512]{1,0:T(8,128)(2,1)}, u32[]{:S(2)}, u32[]{:S(2)}) collective-permute-start(bf16[320,512]{1,0:T(8,128)(2,1)S(1)} %copy-done.5), channel_id=1, source_target_pairs={{3,0},{0,1},{1,2},{2,3},{7,4},{4,5},{5,6},{6,7},{11,8},{8,9},{9,10... | collective-permute-start | bytes 983048 | tf_op jit(solution)/shard_map/ppermute | solution.py:205
  21.1 26.6 %copy-start.7 = (s32[3,2304]{1,0:T(4,128)S(1)}, s32[3,2304]{1,0:T(4,128)}, u32[]{:S(2)}) copy-start(s32[3,2304]{1,0:T(4,128)} %param.13) | copy-start | bytes 82948
  44.0 3.7 %copy-start.2 = (bf16[32,24,768]{2,1,0:T(8,128)(2,1)}, bf16[32,24,768]{2,1,0:T(8,128)(2,1)S(1)}, u32[]{:S(2)}) copy-start(bf16[32,24,768]{2,1,0:T(8,128)(2,1)S(1)} %all-to-all-done) | copy-start | bytes 3538948
  44.0 32.7 %all-to-all-start.2 = ((bf16[32,24,768]{2,1,0:T(8,128)(2,1)}), bf16[32,24,768]{2,1,0:T(8,128)(2,1)}, u32[]{:S(2)}, u32[]{:S(2)}) async-start(bf16[32,24,768]{2,1,0:T(8,128)(2,1)} %bitcast.35), calls=%async_computation.2 | async-start | bytes 2359296 | tf_op jit(solution)/shard_map/all_to_all | solution.py:201
  48.6 1.3 copy-start.1
  48.6 1.5 copy-start.4
  54.5 2.0 copy-start.6
  76.7 32.6 %all-to-all-start.1 = ((bf16[32,24,768]{2,1,0:T(8,128)(2,1)}), bf16[32,24,768]{2,1,0:T(8,128)(2,1)S(1)}, u32[]{:S(2)}, u32[]{:S(2)}) async-start(bf16[32,24,768]{2,1,0:T(8,128)(2,1)} %bitcast.37), calls=%async_computation.1 | async-start | bytes 2359296 | tf_op jit(solution)/shard_map/all_to_all | solution.py:201
  109.4 1.1 copy-start.3
  166.2 35.6 %all-to-all-start.4 = ((bf16[32,40,512]{2,1,0:T(8,128)(2,1)}), bf16[32,40,512]{2,1,0:T(8,128)(2,1)S(1)}, u32[]{:S(2)}, u32[]{:S(2)}) async-start(bf16[32,40,512]{2,1,0:T(8,128)(2,1)} %total.1), calls=%async_computation.4 | async-start | bytes 2621440 | tf_op jit(solution)/shard_map/all_to_all | solution.py:201
  170.1 19.2 %collective-permute-start.3 = (bf16[320,512]{1,0:T(8,128)(2,1)S(1)}, bf16[320,512]{1,0:T(8,128)(2,1)S(1)}, u32[]{:S(2)}, u32[]{:S(2)}) collective-permute-start(bf16[320,512]{1,0:T(8,128)(2,1)S(1)} %get-tuple-element.26), channel_id=1, source_target_pairs={{3,0},{0,1},{1,2},{2,3},{7,4},{4,5},{5,6},{6,7},{11,8},{8,9},{9,10... | collective-permute-start | bytes 983048 | tf_op jit(solution)/shard_map/ppermute | solution.py:205
  170.2 19.5 %collective-permute-start.5 = (bf16[320,512]{1,0:T(8,128)(2,1)S(1)}, bf16[320,512]{1,0:T(8,128)(2,1)S(1)}, u32[]{:S(2)}, u32[]{:S(2)}) collective-permute-start(bf16[320,512]{1,0:T(8,128)(2,1)S(1)} %get-tuple-element.27), channel_id=1, source_target_pairs={{1,0},{2,1},{3,2},{0,3},{5,4},{6,5},{7,6},{4,7},{9,8},{10,9},{11,1... | collective-permute-start | bytes 983048 | tf_op jit(solution)/shard_map/ppermute | solution.py:205
  171.9 27.8 %collective-permute-start.4 = (bf16[320,512]{1,0:T(8,128)(2,1)S(1)}, bf16[320,512]{1,0:T(8,128)(2,1)S(1)}, u32[]{:S(2)}, u32[]{:S(2)}) collective-permute-start(bf16[320,512]{1,0:T(8,128)(2,1)S(1)} %get-tuple-element.28), channel_id=1, source_target_pairs={{2,0},{3,1},{0,2},{1,3},{6,4},{7,5},{4,6},{5,7},{10,8},{11,9},{8,1... | collective-permute-start | bytes 983048 | tf_op jit(solution)/shard_map/ppermute | solution.py:205

commit v3 on v2

--- a/solution.py
+++ b/solution.py
@@ -8,7 +8,8 @@
 from jax.experimental.pallas import tpu as pltpu
 from jax.sharding import PartitionSpec as P
 
-CHUNKS = 3
+CHUNK_ENDS = (4, 7, 9)
+CHUNKS = len(CHUNK_ENDS)
 LANES = 128
 
 
@@ -108,19 +109,23 @@
     grid_part[...] += dot(latent, proj_grad.astype(jnp.bfloat16), 0, 0)
 
     if last:
-        patch_latent, stack, node_sent = refs[9:12]
+        patch_latent, stack = refs[9:11]
+        node_blocks = refs[11:-3]
         extra = outer.shape[0]
 
         @pl.when(pl.program_id(0) == pl.num_programs(0) - 1)
         def _():
-            node_sent[...] = node_part[...].astype(jnp.bfloat16)
+            node_sent = node_part[...].astype(jnp.bfloat16)
+            size = node_blocks[0].shape[0]
+            for member, block in enumerate(node_blocks):
+                block[...] = node_sent[member * size : (member + 1) * size, :]
             stack[:extra, :] = outer[...].astype(jnp.bfloat16)
             stack[extra : extra + width, :] = grid_part[...].astype(jnp.bfloat16)
-            mesh_part = dot(patch_latent[...], node_sent[...], 0, 0)
+            mesh_part = dot(patch_latent[...], node_sent, 0, 0)
             stack[extra + width :, :] = mesh_part.astype(jnp.bfloat16)
 
 
-def edges(rows_in, columns, lanes, table, w_grid, w_both, previous, patch_latent):
+def edges(rows_in, columns, lanes, table, w_grid, w_both, previous, patch_latent, members):
     rows, row_width = rows_in.shape
     nodes, width = table.shape
     extra = row_width - width
@@ -148,7 +153,7 @@
         operands.append(patch_latent)
         out_shape = [
             jax.ShapeDtypeStruct(shape, jnp.bfloat16)
-            for shape in ((extra + 2 * width, width), (nodes, width))
+            for shape in ((extra + 2 * width, width),) + ((nodes // members, width),) * members
         ]
         scratch = [pltpu.VMEM(shape, jnp.float32) for shape in shapes]
     return pl.pallas_call(
@@ -168,19 +173,31 @@
     )(*operands)
 
 
-def total_body(parts, out):
-    total = parts[0].astype(jnp.float32)
-    for part in range(1, parts.shape[0]):
-        total = total + parts[part].astype(jnp.float32)
-    total = total.astype(jnp.bfloat16)
+def sum_of(blocks):
+    total = blocks[0].astype(jnp.float32)
+    for block in blocks[1:]:
+        total = total + block.astype(jnp.float32)
+    return total.astype(jnp.bfloat16)
+
+
+def total_body(parts, *refs):
+    out, node_out = refs[-2:]
+    node_out[...] = sum_of([block[...] for block in refs[:-2]])
+    total = sum_of([parts[part] for part in range(parts.shape[0])])
     for part in range(parts.shape[0]):
         out[part] = total
 
 
-def total_for_all(parts):
+def total_for_all(parts, node_blocks):
+    node = node_blocks[0]
     return pl.pallas_call(
-        total_body, out_shape=jax.ShapeDtypeStruct(parts.shape, parts.dtype), name="total"
-    )(parts)
+        total_body,
+        out_shape=[
+            jax.ShapeDtypeStruct(parts.shape, parts.dtype),
+            jax.ShapeDtypeStruct(node.shape, node.dtype),
+        ],
+        name="total",
+    )(parts, *node_blocks)
 
 
 def shards(grad_pred, grid_latent, mesh_latent, send_slot, edge_src, w_mesh, w_grid, w_msg, w_out):
@@ -194,8 +211,8 @@
     total_points = grid_rows * devices
     patch_size = members * mesh_rows
     extra = -(-channels // LANES) * LANES
-    step = capacity // CHUNKS
-    chunk_rows = devices * step
+    ends = [capacity * end // CHUNK_ENDS[-1] for end in CHUNK_ENDS]
+    spans = list(zip([0] + ends[:-1], ends))
 
     def exchange(blocks):
         return lax.all_to_all(blocks, axes, split_axis=0, concat_axis=0, tiled=True)
@@ -209,54 +226,58 @@
     )
     first_node = lax.axis_index(axes) * mesh_rows
     local = (edge_src - first_node) % patch_size
-    local = local.reshape(3, devices, CHUNKS, step).transpose(2, 0, 1, 3)
-    local = local.reshape(CHUNKS, 3, chunk_rows)
-    local_columns = local.transpose(0, 2, 1)
+    local = local.reshape(3, devices, capacity)
+    local = [local[:, :, start:end].reshape(3, -1) for start, end in spans]
     w_both = jnp.pad(
         dot(w_msg, w_out, 1, 0).astype(jnp.bfloat16), ((0, 0), (0, extra - channels))
     )
     table = dot(patch_latent, w_mesh, 1, 0).astype(jnp.bfloat16)
 
     points = lax.axis_index(axes) * grid_rows + jnp.arange(grid_rows, dtype=jnp.int32)
+    padded = jnp.pad(grad_pred, ((0, extra - channels), (0, 0)))
     weighted = (
-        latitude_weight(points, total_points)[None, :] * grad_pred.astype(jnp.float32)
+        latitude_weight(points, total_points)[None, :] * padded.astype(jnp.float32)
     ).astype(jnp.bfloat16)
-    weighted = jnp.pad(weighted, ((0, extra - channels), (0, 0)))
     target = send_slot // capacity
     rank = send_slot % capacity
-    place = (rank // step) * chunk_rows + target * step + rank % step
+    place = None
+    for start, end in reversed(spans):
+        here = start * devices + target * (end - start) + rank - start
+        place = here if place is None else jnp.where(rank < end, here, place)
     place = place[None, :]
 
     def send(chunk, after):
-        packed = pack(place, grid_latent, weighted, chunk * chunk_rows, chunk_rows, after)
-        arrived = exchange(packed.reshape(devices, step, width + extra))
-        return arrived.reshape(chunk_rows, width + extra)
+        start, end = spans[chunk]
+        rows = devices * (end - start)
+        packed = pack(place, grid_latent, weighted, start * devices, rows, after)
+        arrived = exchange(packed.reshape(devices, end - start, width + extra))
+        return arrived.reshape(rows, width + extra)
 
     arrived = [send(chunk, None) for chunk in range(min(2, CHUNKS))]
     sums = None
     for chunk in range(CHUNKS):
         sums = edges(
             arrived[chunk],
-            local_columns[chunk],
+            local[chunk].T,
             local[chunk],
             table,
             w_grid,
             w_both,
             sums,
             patch_latent if chunk == CHUNKS - 1 else None,
+            members,
         )
         if chunk + 2 < CHUNKS:
             arrived.append(send(chunk + 2, sums[0]))
-    stack, node_sent = sums
-
+    stack, *node_blocks = sums
+
+    node_blocks = [node_blocks[0]] + [
+        from_member(node_blocks[shift], -shift) for shift in range(1, members)
+    ]
     shares = exchange(stack.reshape(devices, stack.shape[0] // devices, width))
-    node_blocks = node_sent.reshape(members, mesh_rows, width)
-    node_total = node_blocks[0].astype(jnp.float32)
-    for shift in range(1, members):
-        node_total = node_total + from_member(node_blocks[shift], -shift).astype(jnp.float32)
-    mesh_proj_grad = node_total.astype(jnp.bfloat16)
+    totals, mesh_proj_grad = total_for_all(shares, node_blocks)
     mesh_grad = dot(mesh_proj_grad, w_mesh, 1, 1).astype(jnp.bfloat16)
-    totals = exchange(total_for_all(shares)).reshape(stack.shape)
+    totals = exchange(totals).reshape(stack.shape)
     grad_scale = 1.0 / math.sqrt(3.0 * total_points)
     outer_total = totals[:channels]
     out_total = dot(w_msg, outer_total, 0, 1)

time: 207 us -> 204 us (0.986)
  blocking collectives: 36.9 us -> 0 us
  waiting for transfers between devices: 63.7 us -> 94.9 us
  starting transfers between devices: 23.3 us -> 28.6 us
  local copies, waits for them, and re-layouts: 11.4 us -> 8.97 us
    all_to_all x1 -> x0, blocking collectives: 36.9 us -> none  [exchange(): return lax.all_to_all(blocks, axes, split_axis=0, concat_axis=0, tiled=True)]
    all_to_all x4 -> x5, waiting for transfers between devices: 37.5 us -> 69.2 us  [exchange(): return lax.all_to_all(blocks, axes, split_axis=0, concat_axis=0, tiled=True)]
    all_to_all x4 -> x5, starting transfers between devices: 17.5 us -> 23.3 us  [exchange(): return lax.all_to_all(blocks, axes, split_axis=0, concat_axis=0, tiled=True)]
    squeeze x4 -> x0, local copies, waits for them, and re-layouts: 3.11 us -> none  [the longest x3 2.07 us: shards(): local[chunk]]
  transfers between devices with their start and end apart: 10 -> 11, of which waited for: 6 -> 8; matrix products, arithmetic and copies ran while one was open for 6% -> 5% of each run, Pallas kernels for 18% -> 19%
where the time goes in v3:
time: 204 us; the launch traced here: 203 us
  waiting for transfers between devices  94.9 us (47%)
  Pallas kernels  59.7 us (29%)
  starting transfers between devices  28.6 us (14%)
  local copies, waits for them, and re-layouts  8.97 us (4%)
  matrix products  5.69 us (3%)
  other arithmetic  4.26 us (2%)
    all_to_all x5, waiting for transfers between devices, exchange(): return lax.all_to_all(blocks, axes, split_axis=0, concat_axis=0, tiled=True)  69.2 us
    pallas_call x3, Pallas kernels, edges(): pl.pallas_call(functools.partial(edge_body, width=width, chained=chained,...  45.4 us
    ppermute x6, waiting for transfers between devices, from_member(): return lax.ppermute(block, 'sub', pairs)  25.7 us
    all_to_all x5, starting transfers between devices, exchange(): return lax.all_to_all(blocks, axes, split_axis=0, concat_axis=0, tiled=True)  23.3 us
    pallas_call x3, Pallas kernels, pack(): pl.pallas_call(functools.partial(pack_body, block=block, width=width, bas...  11.1 us
    dot_general x5, matrix products, dot(): lax.dot_general(left, right, (((left_dim,), (right_dim,)), ((), ())), pre...  5.69 us
    ppermute x6, starting transfers between devices, from_member(): return lax.ppermute(block, 'sub', pairs)  5.27 us
  transfers between devices with their start and end apart: 11, of which 8 were waited for; matrix products, arithmetic and copies ran while one was open for 5% of the time, Pallas kernels for 19%

profile of v3, /device:TPU:0, one launch (start us, length us, event | category | flops | bytes accessed | tf_op | source)
XLA Modules:
  0.0 202.9 jit_solution(13902910093884741905)
XLA Ops:
  2.1 1.8 multiply_convert_fusion.weighted
  3.8 4.3 %pack.3 = bf16[1024,768]{1,0:T(8,128)(2,1)} custom-call(s32[1,768]{1,0:T(1,128)} %broadcast_in_dim.4.place, bf16[768,512]{1,0:T(8,128)(2,1)} %latent.5, bf16[256,768]{1,0:T(8,128)(2,1)} %multiply_convert_fusion.weighted), custom_call_target="tpu_custom_call" | custom-call | flops 1207959552 | bytes 3145728 | tf_op jit(solution)/shard_map/pack/pallas_call | solution.py:59
  8.1 7.4 %all-to-all-start = ((bf16[32,32,768]{2,1,0:T(8,128)(2,1)}), bf16[32,32,768]{2,1,0:T(8,128)(2,1)}, u32[]{:S(2)}, u32[]{:S(2)}) async-start(bf16[32,32,768]{2,1,0:T(8,128)(2,1)} %bitcast.26), calls=%async_computation | async-start | bytes 3145728 | tf_op jit(solution)/shard_map/all_to_all | solution.py:218
  15.6 1.5 collective-permute-start
  17.6 3.8 %pack.5 = bf16[768,768]{1,0:T(8,128)(2,1)} custom-call(s32[1,768]{1,0:T(1,128)} %broadcast_in_dim.4.place, bf16[768,512]{1,0:T(8,128)(2,1)} %latent.5, bf16[256,768]{1,0:T(8,128)(2,1)} %multiply_convert_fusion.weighted), custom_call_target="tpu_custom_call" | custom-call | flops 905969664 | bytes 2359296 | tf_op jit(solution)/shard_map/pack/pallas_call | solution.py:59
  21.4 31.6 %all-to-all-done = bf16[32,32,768]{2,1,0:T(8,128)(2,1)} async-done(((bf16[32,32,768]{2,1,0:T(8,128)(2,1)}), bf16[32,32,768]{2,1,0:T(8,128)(2,1)}, u32[]{:S(2)}, u32[]{:S(2)}) %all-to-all-start) | async-done | bytes 1572896 | tf_op jit(solution)/shard_map/all_to_all | solution.py:218
  53.0 3.6 %all-to-all-start.2 = ((bf16[32,24,768]{2,1,0:T(8,128)(2,1)}), bf16[32,24,768]{2,1,0:T(8,128)(2,1)S(1)}, u32[]{:S(2)}, u32[]{:S(2)}) async-start(bf16[32,24,768]{2,1,0:T(8,128)(2,1)} %bitcast.29), calls=%async_computation.2 | async-start | bytes 2359296 | tf_op jit(solution)/shard_map/all_to_all | solution.py:218
  57.3 1.0 copy.23.refs_1_
  59.2 1.0 constant_dynamic-update-slice_fusion.2
  62.3 1.9 convolution_convert_fusion.refs_3_
  64.2 17.3 %edges.3 = (f32[256,512]{1,0:T(8,128)}, f32[512,512]{1,0:T(8,128)}, f32[1280,512]{1,0:T(8,128)}) custom-call(bf16[1024,768]{1,0:T(8,128)(2,1)} %bitcast.1.refs_0_, s32[1024,3]{1,0:T(8,128)} %copy.23.refs_1_, s32[3,1024]{1,0:T(4,128)} %copy-done.10, bf16[1280,512]{1,0:T(8,128)(2,1)} %convolution_convert_fusion.refs_3_, bf16[512,512]{1,0:T(8,128)(2,1)} %refs_4_.5, ...), custom_call_target="tpu_custom_call" | custom-call | flops 9663676416 | bytes 12058624 | tf_op jit(solution)/shard_map/edges/pallas_call | solution.py:159
  81.5 3.0 %pack.4 = bf16[512,768]{1,0:T(8,128)(2,1)} custom-call(s32[1,768]{1,0:T(1,128)} %broadcast_in_dim.4.place, bf16[768,512]{1,0:T(8,128)(2,1)} %latent.5, bf16[256,768]{1,0:T(8,128)(2,1)} %multiply_convert_fusion.weighted, f32[256,512]{1,0:T(8,128)} %get-tuple-element.18.rest_0_.refs_6_), custom_call_target="tpu_custom_call" | custom-call | flops 603979776 | bytes 1572864 | tf_op jit(solution)/shard_map/pack/pallas_call | solution.py:59
  84.5 1.1 all-to-all-done.2
  85.7 5.0 %all-to-all-start.1 = ((bf16[32,16,768]{2,1,0:T(8,128)(2,1)}), bf16[32,16,768]{2,1,0:T(8,128)(2,1)}, u32[]{:S(2)}, u32[]{:S(2)}) async-start(bf16[32,16,768]{2,1,0:T(8,128)(2,1)} %bitcast.25), calls=%async_computation.1 | async-start | bytes 1572864 | tf_op jit(solution)/shard_map/all_to_all | solution.py:218
  92.8 15.3 %edges.4 = (f32[256,512]{1,0:T(8,128)}, f32[512,512]{1,0:T(8,128)}, f32[1280,512]{1,0:T(8,128)}) custom-call(bf16[768,768]{1,0:T(8,128)(2,1)} %bitcast.28, s32[768,3]{1,0:T(8,128)} %bitcast.31, s32[3,768]{1,0:T(4,128)} %copy-done.11, bf16[1280,512]{1,0:T(8,128)(2,1)} %convolution_convert_fusion.refs_3_, bf16[512,512]{1,0:T(8,128)(2,1)} %refs_4_.5, ...), custom_call_target="tpu_custom_call" | custom-call | flops 7247757312 | bytes 11665408 | tf_op jit(solution)/shard_map/edges/pallas_call | solution.py:159
  108.2 2.9 %all-to-all-done.1 = bf16[32,16,768]{2,1,0:T(8,128)(2,1)} async-done(((bf16[32,16,768]{2,1,0:T(8,128)(2,1)}), bf16[32,16,768]{2,1,0:T(8,128)(2,1)}, u32[]{:S(2)}, u32[]{:S(2)}) %all-to-all-start.1) | async-done | bytes 786464 | tf_op jit(solution)/shard_map/all_to_all | solution.py:218
  111.1 12.8 %edges.5 = (bf16[1280,512]{1,0:T(8,128)(2,1)}, bf16[320,512]{1,0:T(8,128)(2,1)}, bf16[320,512]{1,0:T(8,128)(2,1)}, bf16[320,512]{1,0:T(8,128)(2,1)}, bf16[320,512]{1,0:T(8,128)(2,1)}) custom-call(bf16[512,768]{1,0:T(8,128)(2,1)} %bitcast.4.refs_0_, s32[512,3]{1,0:T(8,128)} %bitcast.32, s32[3,512]{1,0:T(4,128)} %copy-done.13, ...), custom_call_target="tpu_custom_call" | custom-call | flops 4831838208 | bytes 11272192 | tf_op jit(solution)/shard_map/edges/pallas_call | solution.py:159
  123.8 3.6 %all-to-all-start.3 = ((bf16[32,40,512]{2,1,0:T(8,128)(2,1)}), bf16[32,40,512]{2,1,0:T(8,128)(2,1)S(1)}, u32[]{:S(2)}, u32[]{:S(2)}) async-start(bf16[32,40,512]{2,1,0:T(8,128)(2,1)} %bitcast.27), calls=%async_computation.3 | async-start | bytes 2621440 | tf_op jit(solution)/shard_map/all_to_all | solution.py:218
  127.8 1.6 collective-permute-start.4
  129.4 1.4 collective-permute-start.5
  130.8 17.8 %collective-permute-done.3.refs_1_ = bf16[320,512]{1,0:T(8,128)(2,1)S(1)} collective-permute-done((bf16[320,512]{1,0:T(8,128)(2,1)}, bf16[320,512]{1,0:T(8,128)(2,1)S(1)}, u32[]{:S(2)}, u32[]{:S(2)}) %collective-permute-start.3) | collective-permute-done | bytes 327712 | tf_op jit(solution)/shard_map/ppermute | solution.py:222
  148.6 1.2 collective-permute-done.4.refs_2_
  149.7 6.7 %collective-permute-done.5.refs_3_ = bf16[320,512]{1,0:T(8,128)(2,1)} collective-permute-done((bf16[320,512]{1,0:T(8,128)(2,1)}, bf16[320,512]{1,0:T(8,128)(2,1)}, u32[]{:S(2)}, u32[]{:S(2)}) %collective-permute-start.5) | collective-permute-done | bytes 327712 | tf_op jit(solution)/shard_map/ppermute | solution.py:222
  156.4 2.9 %all-to-all-done.3.parts = bf16[32,40,512]{2,1,0:T(8,128)(2,1)S(1)} async-done(((bf16[32,40,512]{2,1,0:T(8,128)(2,1)}), bf16[32,40,512]{2,1,0:T(8,128)(2,1)S(1)}, u32[]{:S(2)}, u32[]{:S(2)}) %all-to-all-start.3) | async-done | bytes 1310752 | tf_op jit(solution)/shard_map/all_to_all | solution.py:218
  159.3 1.1 copy-done.1
  160.4 3.1 %total.1 = (bf16[32,40,512]{2,1,0:T(8,128)(2,1)}, bf16[320,512]{1,0:T(8,128)(2,1)}) custom-call(bf16[32,40,512]{2,1,0:T(8,128)(2,1)} %copy-done.1, bf16[320,512]{1,0:T(8,128)(2,1)} %get-tuple-element.25.refs_0_, bf16[320,512]{1,0:T(8,128)(2,1)} %copy-done.5, bf16[320,512]{1,0:T(8,128)(2,1)} %copy-done.6, bf16[320,512]{1,0:T(8,128)(2,1)} %collective-permute-done.5.refs_3_), custom_call_target="tpu_custom_call" | custom-call | tf_op jit(solution)/shard_map/total/pallas_call | solution.py:193
  163.5 3.6 %all-to-all-start.4 = ((bf16[32,40,512]{2,1,0:T(8,128)(2,1)}), bf16[32,40,512]{2,1,0:T(8,128)(2,1)S(1)}, u32[]{:S(2)}, u32[]{:S(2)}) async-start(bf16[32,40,512]{2,1,0:T(8,128)(2,1)} %get-tuple-element.30), calls=%async_computation.4 | async-start | bytes 2621440 | tf_op jit(solution)/shard_map/all_to_all | solution.py:218
  167.1 1.1 convolution_convert_fusion.1
  168.2 30.7 %all-to-all-done.4 = bf16[32,40,512]{2,1,0:T(8,128)(2,1)S(1)} async-done(((bf16[32,40,512]{2,1,0:T(8,128)(2,1)}), bf16[32,40,512]{2,1,0:T(8,128)(2,1)S(1)}, u32[]{:S(2)}, u32[]{:S(2)}) %all-to-all-start.4) | async-done | bytes 1310752 | tf_op jit(solution)/shard_map/all_to_all | solution.py:218
  198.9 1.6 convert_multiply_fusion
  200.6 1.3 convolution_multiply_fusion
  201.9 1.1 fusion
  (51 shorter events, 7.9 us)
Async XLA Ops:
  0.6 61.6 %copy-start = (bf16[512,512]{1,0:T(8,128)(2,1)S(1)}, bf16[512,512]{1,0:T(8,128)(2,1)}, u32[]{:S(2)}) copy-start(bf16[512,512]{1,0:T(8,128)(2,1)} %param.14) | copy-start | bytes 1572868
  8.1 7.5 %copy-start.8 = (bf16[320,512]{1,0:T(8,128)(2,1)S(1)}, bf16[320,512]{1,0:T(8,128)(2,1)}, u32[]{:S(2)}) copy-start(bf16[320,512]{1,0:T(8,128)(2,1)} %param.11) | copy-start | bytes 983044
  8.1 44.9 %all-to-all-start = ((bf16[32,32,768]{2,1,0:T(8,128)(2,1)}), bf16[32,32,768]{2,1,0:T(8,128)(2,1)}, u32[]{:S(2)}, u32[]{:S(2)}) async-start(bf16[32,32,768]{2,1,0:T(8,128)(2,1)} %bitcast.26), calls=%async_computation | async-start | bytes 3145728 | tf_op jit(solution)/shard_map/all_to_all | solution.py:218
  15.6 43.6 %collective-permute-start = (bf16[320,512]{1,0:T(8,128)(2,1)S(1)}, bf16[320,512]{1,0:T(8,128)(2,1)}, u32[]{:S(2)}, u32[]{:S(2)}) collective-permute-start(bf16[320,512]{1,0:T(8,128)(2,1)S(1)} %copy-done.8), channel_id=1, source_target_pairs={{1,0},{2,1},{3,2},{0,3},{5,4},{6,5},{7,6},{4,7},{9,8},{10,9},{11,1... | collective-permute-start | bytes 983048 | tf_op jit(solution)/shard_map/ppermute | solution.py:222
  17.1 43.2 %collective-permute-start.1 = (bf16[320,512]{1,0:T(8,128)(2,1)S(1)}, bf16[320,512]{1,0:T(8,128)(2,1)}, u32[]{:S(2)}, u32[]{:S(2)}) collective-permute-start(bf16[320,512]{1,0:T(8,128)(2,1)S(1)} %copy-done.8), channel_id=1, source_target_pairs={{2,0},{3,1},{0,2},{1,3},{6,4},{7,5},{4,6},{5,7},{10,8},{11,9},{8,1... | collective-permute-start | bytes 983048 | tf_op jit(solution)/shard_map/ppermute | solution.py:222
  17.5 43.8 %collective-permute-start.2 = (bf16[320,512]{1,0:T(8,128)(2,1)S(1)}, bf16[320,512]{1,0:T(8,128)(2,1)}, u32[]{:S(2)}, u32[]{:S(2)}) collective-permute-start(bf16[320,512]{1,0:T(8,128)(2,1)S(1)} %copy-done.8), channel_id=1, source_target_pairs={{3,0},{0,1},{1,2},{2,3},{7,4},{4,5},{5,6},{6,7},{11,8},{8,9},{9,10... | collective-permute-start | bytes 983048 | tf_op jit(solution)/shard_map/ppermute | solution.py:222
  21.4 35.2 %copy-start.12 = (s32[3,2304]{1,0:T(4,128)S(1)}, s32[3,2304]{1,0:T(4,128)}, u32[]{:S(2)}) copy-start(s32[3,2304]{1,0:T(4,128)} %param.13) | copy-start | bytes 82948
  21.4 35.3 %copy-start.2 = (bf16[512,512]{1,0:T(8,128)(2,1)S(1)}, bf16[512,512]{1,0:T(8,128)(2,1)}, u32[]{:S(2)}) copy-start(bf16[512,512]{1,0:T(8,128)(2,1)} %param.16) | copy-start | bytes 1572868
  21.4 35.3 %copy-start.4 = (bf16[512,227]{0,1:T(8,128)(2,1)S(1)}, bf16[512,227]{0,1:T(8,128)(2,1)}, u32[]{:S(2)}) copy-start(bf16[512,227]{0,1:T(8,128)(2,1)} %param.17) | copy-start | bytes 697348
  53.0 32.6 %all-to-all-start.2 = ((bf16[32,24,768]{2,1,0:T(8,128)(2,1)}), bf16[32,24,768]{2,1,0:T(8,128)(2,1)S(1)}, u32[]{:S(2)}, u32[]{:S(2)}) async-start(bf16[32,24,768]{2,1,0:T(8,128)(2,1)} %bitcast.29), calls=%async_computation.2 | async-start | bytes 2359296 | tf_op jit(solution)/shard_map/all_to_all | solution.py:218
  57.3 2.9 %copy-start.10 = (s32[3,1024]{1,0:T(4,128)}, s32[3,1024]{1,0:T(4,128)S(1)}, u32[]{:S(2)}) copy-start(s32[3,1024]{1,0:T(4,128)S(1)} %reshape.60.refs_2_) | copy-start | bytes 36868
  62.2 1.9 copy-start.9
  85.7 7.2 %copy-start.3 = (bf16[32,24,768]{2,1,0:T(8,128)(2,1)}, bf16[32,24,768]{2,1,0:T(8,128)(2,1)S(1)}, u32[]{:S(2)}) copy-start(bf16[32,24,768]{2,1,0:T(8,128)(2,1)S(1)} %all-to-all-done.2) | copy-start | bytes 3538948
  85.7 25.4 %all-to-all-start.1 = ((bf16[32,16,768]{2,1,0:T(8,128)(2,1)}), bf16[32,16,768]{2,1,0:T(8,128)(2,1)}, u32[]{:S(2)}, u32[]{:S(2)}) async-start(bf16[32,16,768]{2,1,0:T(8,128)(2,1)} %bitcast.25), calls=%async_computation.1 | async-start | bytes 1572864 | tf_op jit(solution)/shard_map/all_to_all | solution.py:218
  90.9 1.9 copy-start.11
  92.0 16.2 %copy-start.13 = (s32[3,512]{1,0:T(4,128)}, s32[3,512]{1,0:T(4,128)S(1)}, u32[]{:S(2)}) copy-start(s32[3,512]{1,0:T(4,128)S(1)} %reshape.63.refs_2_) | copy-start | bytes 18436
  123.8 35.5 %all-to-all-start.3 = ((bf16[32,40,512]{2,1,0:T(8,128)(2,1)}), bf16[32,40,512]{2,1,0:T(8,128)(2,1)S(1)}, u32[]{:S(2)}, u32[]{:S(2)}) async-start(bf16[32,40,512]{2,1,0:T(8,128)(2,1)} %bitcast.27), calls=%async_computation.3 | async-start | bytes 2621440 | tf_op jit(solution)/shard_map/all_to_all | solution.py:218
  127.5 21.1 %collective-permute-start.3 = (bf16[320,512]{1,0:T(8,128)(2,1)}, bf16[320,512]{1,0:T(8,128)(2,1)S(1)}, u32[]{:S(2)}, u32[]{:S(2)}) collective-permute-start(bf16[320,512]{1,0:T(8,128)(2,1)} %get-tuple-element.26), channel_id=1, source_target_pairs={{3,0},{0,1},{1,2},{2,3},{7,4},{4,5},{5,6},{6,7},{11,8},{8,9},{9,10... | collective-permute-start | bytes 983048 | tf_op jit(solution)/shard_map/ppermute | solution.py:222
  127.8 22.0 %collective-permute-start.4 = (bf16[320,512]{1,0:T(8,128)(2,1)}, bf16[320,512]{1,0:T(8,128)(2,1)S(1)}, u32[]{:S(2)}, u32[]{:S(2)}) collective-permute-start(bf16[320,512]{1,0:T(8,128)(2,1)} %get-tuple-element.27), channel_id=1, source_target_pairs={{2,0},{3,1},{0,2},{1,3},{6,4},{7,5},{4,6},{5,7},{10,8},{11,9},{8,1... | collective-permute-start | bytes 983048 | tf_op jit(solution)/shard_map/ppermute | solution.py:222
  129.4 27.0 %collective-permute-start.5 = (bf16[320,512]{1,0:T(8,128)(2,1)}, bf16[320,512]{1,0:T(8,128)(2,1)}, u32[]{:S(2)}, u32[]{:S(2)}) collective-permute-start(bf16[320,512]{1,0:T(8,128)(2,1)} %get-tuple-element.28), channel_id=1, source_target_pairs={{1,0},{2,1},{3,2},{0,3},{5,4},{6,5},{7,6},{4,7},{9,8},{10,9},{11,1... | collective-permute-start | bytes 983048 | tf_op jit(solution)/shard_map/ppermute | solution.py:222
  148.6 10.7 %copy-start.5 = (bf16[320,512]{1,0:T(8,128)(2,1)}, bf16[320,512]{1,0:T(8,128)(2,1)S(1)}, u32[]{:S(2)}) copy-start(bf16[320,512]{1,0:T(8,128)(2,1)S(1)} %collective-permute-done.3.refs_1_) | copy-start | bytes 983044
  149.7 9.6 %copy-start.6 = (bf16[320,512]{1,0:T(8,128)(2,1)}, bf16[320,512]{1,0:T(8,128)(2,1)S(1)}, u32[]{:S(2)}) copy-start(bf16[320,512]{1,0:T(8,128)(2,1)S(1)} %collective-permute-done.4.refs_2_) | copy-start | bytes 983044
  159.3 1.1 copy-start.1
  163.5 3.6 %copy-start.7 = (bf16[320,512]{1,0:T(8,128)(2,1)S(1)}, bf16[320,512]{1,0:T(8,128)(2,1)}, u32[]{:S(2)}) copy-start(bf16[320,512]{1,0:T(8,128)(2,1)} %get-tuple-element.29) | copy-start | bytes 983044
  163.5 35.4 %all-to-all-start.4 = ((bf16[32,40,512]{2,1,0:T(8,128)(2,1)}), bf16[32,40,512]{2,1,0:T(8,128)(2,1)S(1)}, u32[]{:S(2)}, u32[]{:S(2)}) async-start(bf16[32,40,512]{2,1,0:T(8,128)(2,1)} %get-tuple-element.30), calls=%async_computation.4 | async-start | bytes 2621440 | tf_op jit(solution)/shard_map/all_to_all | solution.py:218
